TPU v7x, 32 devices: a whole 2x2x4 slice. The times are simulated.
32 devices in a mesh: dp: 4 (over z), head: 2 (over y), tok: 4 (over x, core).
Axes of the slice: x: 2, y: 2, z: 4, core: 2. Of those that a mesh axis runs over, the one named last changes fastest.
Arguments:
- mamba_input: bfloat16 [8, 64, 2048], P('dp', 'tok', 'head'), may hold values from -6 to 6
- gate_input: bfloat16 [8, 64, 2048], P('dp', 'tok', 'head'), may hold values from -6 to 6
- in_b: bfloat16 [8, 64, 256], P('dp', 'tok', 'head'), may hold values from -0.75 to 0.75
- in_c: bfloat16 [8, 64, 256], P('dp', 'tok', 'head'), may hold values from -0.75 to 0.75
- step_size: bfloat16 [8, 64, 32], P('dp', 'tok', 'head'), may hold values from 0.019897461 to 1
- decay_rate: float32 [32], P('head'), may hold values from 0.01 to 1
- skip_weight: float32 [32], P('head'), may hold values from 0.5 to 1.5
- norm_gain: float32 [2048], P('head'), may hold values from 0.1 to 1.9
- ssm_state: bfloat16 [8, 32, 64, 128], P('dp', 'head', None, 'tok'), may hold values from -6 to 6
- out_weight: bfloat16 [2048, 4096], P(('head', 'tok')), may hold values from -0.125 to 0.125
- queries: bfloat16 [8, 64, 1024], P('dp', 'tok', 'head'), may hold values from -6 to 6
- draft_token_keys: bfloat16 [8, 64, 256], P('dp', 'tok', 'head'), may hold values from -6 to 6
- draft_values: bfloat16 [8, 64, 256], P('dp', 'tok', 'head'), may hold values from -6 to 6
- cached_key_rows: bfloat16 [8, 4096, 256], P('dp', 'tok', 'head'), may hold values from -4 to 4
- cache_values: bfloat16 [8, 4096, 256], P('dp', 'tok', 'head'), may hold values from -6 to 6
- cache_len: int32 [8], P('dp'), may hold values from 2 to 4096
- accepted: int32 [8], P('dp'), may hold values from 0 to 64
Outputs:
- mamba_out: bfloat16 [64, 8, 4096], P(('head', 'tok'), 'dp')
- attn_context: bfloat16 [8, 64, 1024], P('dp', 'tok', 'head')
- committed_state: bfloat16 [8, 32, 64, 128], P('dp', 'head', None, 'tok')
Inputs may be any that keep to these rules, and one draw needn't show every extreme that they name: Each sequence's cached positions 0 to cache_len - 1 are valid.
All inputs are finite; a program needn't handle non-finite values.
Results may differ from a plain program's by a relative error of at most 0.018.
Values may be sent and summed in bfloat16 or wider, within the bound.
A program may use at most 64 MiB of HBM per device.

v0:
```python
import functools
import jax
import jax.numpy as jnp
from jax import lax
from jax.experimental import pallas as pl
from jax.experimental.pallas import tpu as pltpu
from jax.sharding import PartitionSpec as P

EPSILON = 1e-05
MASKED = -1e30
FLOOR = -1e29
MESH = pl.DeviceIdType.MESH
F32 = jnp.float32
BF16 = jnp.bfloat16
NT = (((1,), (1,)), ((), ()))


def dot(a, b):
    return jnp.dot(a, b, preferred_element_type=F32)


def iota(shape, dim):
    return lax.broadcasted_iota(jnp.int32, shape, dim)


def kernel(
    dims,
    x_in, z_in, b_in, c_in, dt_in, st_in, q_in, k_in, v_in, w_in,
    dk_in, dv_in, gain_in, rate_ref, skip_ref, len_ref, acc_ref,
    out_ref, ctx_ref, com_ref,
    x_l, z_l, b_l, c_l, dt_l, st_l, q_l, k_v, v_v, w_v,
    ss_l, cm_s, cm_l, n_s, n_l, stat_l, part, rs_l,
    dk_ref, dv_ref, gain_ref, raw_v, turn_v, pair_l, red,
    send, recv, rs_send, rs_recv, pair_send, pair_recv, local,
):
    n_head, n_tok, seqs, block, heads, chunks = dims
    group = n_head * n_tok
    tok = lax.axis_index("tok")
    head = lax.axis_index("head")
    me = head * n_tok + tok
    draft = block * n_tok
    width = x_l.shape[2]
    own = heads // n_tok
    size = width // own
    state = st_l.shape[1]
    cols = state // n_tok
    att = k_v.shape[2]
    per_kv = q_l.shape[2] // att
    cache = k_v.shape[1]
    rows = seqs * draft
    each = rows // group
    out_cols = w_v.shape[1]
    span = out_cols // chunks

    def place(index, unit):
        return pl.ds(pl.multiple_of(index * unit, unit), unit)

    barrier = pltpu.get_barrier_semaphore()
    for o in range(1, group):
        peer = lax.rem(me + o, group)
        pl.semaphore_signal(
            barrier, inc=1,
            device_id={"head": peer // n_tok, "tok": lax.rem(peer, n_tok)},
            device_id_type=MESH,
        )

    mine = place(tok, block)
    locals_ = [
        (x_in.at[:, :, place(tok, width)], x_l.at[:, mine, :]),
        (z_in.at[:, :, place(tok, width)], z_l.at[:, mine, :]),
        (b_in, b_l.at[:, mine, :]),
        (c_in, c_l.at[:, mine, :]),
        (dt_in, dt_l.at[:, mine, :]),
        (st_in, raw_v),
        (q_in, q_l.at[:, mine, :]),
        (w_in, w_v),
        (k_in, k_v),
        (v_in, v_v),
        (dk_in, dk_ref),
        (dv_in, dv_ref),
        (gain_in, gain_ref),
    ]
    held = [
        pltpu.make_async_copy(src, dst, local.at[i]) for i, (src, dst) in enumerate(locals_)
    ]
    for copy in held:
        copy.start()

    held[5].wait()
    for s in range(seqs):
        turn_v[s] = jnp.concatenate(
            [raw_v[s, h].astype(F32) for h in range(heads)], axis=1
        ).astype(BF16)
    st_l[:, place(tok, cols), :] = turn_v[:, :, place(tok, width)]

    pl.semaphore_wait(barrier, group - 1)

    def remote(kind, o, src, dst):
        return pltpu.make_async_remote_copy(
            src_ref=src, dst_ref=dst,
            send_sem=send.at[kind, o], recv_sem=recv.at[kind, o],
            device_id={"tok": lax.rem(tok + o, n_tok)}, device_id_type=MESH,
        )

    started = []

    def ship(kind, o, src, dst):
        copy = remote(kind, o, src, dst)
        copy.start()
        started.append(copy)

    first = {}
    for o in range(1, n_tok):
        to = lax.rem(tok + o, n_tok)
        pairs = [
            (dt_in, dt_l.at[:, mine, :]),
            (b_in, b_l.at[:, mine, :]),
            (c_in, c_l.at[:, mine, :]),
            (x_in.at[:, :, place(to, width)], x_l.at[:, mine, :]),
            (turn_v.at[:, :, place(to, width)], st_l.at[:, place(tok, cols), :]),
            (z_in.at[:, :, place(to, width)], z_l.at[:, mine, :]),
        ]
        for kind, (src, dst) in enumerate(pairs):
            ship(kind, o, src, dst)
            first[kind, o] = started[-1]
    for o in range(1, n_tok):
        ship(6, o, q_in, q_l.at[:, mine, :])
        first[6, o] = started[-1]

    lane = iota((1, width), 1)
    rate_x = jnp.zeros((1, width), F32)
    skip_x = jnp.zeros((1, width), F32)
    for h in range(own):
        inside = (lane >= h * size) & (lane < (h + 1) * size)
        rate_x = jnp.where(inside, rate_ref[tok * own + h], rate_x)
        skip_x = jnp.where(inside, skip_ref[tok * own + h], skip_x)
    offset = iota((heads, width), 1) - (iota((heads, width), 0) - tok * own) * size
    pick = ((offset >= 0) & (offset < size)).astype(F32).astype(BF16)
    causal = iota((draft, draft), 0) >= iota((draft, draft), 1)
    lower = causal.astype(F32).astype(BF16)

    eye = iota((rows, rows), 0) == iota((rows, rows), 1)
    source = iota((1, rows), 1)
    target = jnp.zeros((1, rows), jnp.int32)
    per = draft // group
    for s in range(seqs):
        for g in range(group):
            start = s * draft + g * per
            base = (g % 2) * (rows // 2) + (g // 2) * each + s
            inside = (source >= start) & (source < start + per)
            target = jnp.where(inside, (source - start) * seqs + base, target)
    swap = (iota((rows, rows), 0) == target).astype(F32).astype(BF16)

    for copy in held[:5]:
        copy.wait()
    for kind in range(6):
        for o in range(1, n_tok):
            first[kind, o].wait_recv()

    gated = []
    saved = []
    for s in range(seqs):
        x = x_l[s].astype(F32)
        z = z_l[s].astype(F32)
        b = b_l[s]
        c = c_l[s]
        st = st_l[s]
        dtx = dot(dt_l[s], pick)
        run = -rate_x * dot(lower, dtx.astype(BF16))
        scaled = (x * dtx * jnp.exp(-run)).astype(BF16)
        mix = lax.dot_general(c, b, NT, preferred_element_type=F32)
        mix = jnp.where(causal, mix, 0.0).astype(BF16)
        y = jnp.exp(run) * (dot(mix, scaled) + dot(c, st)) + skip_x * x
        gated.append(y * z / (1.0 + jnp.exp(-z)))
        saved.append((x, dtx, run))
    gated = jnp.concatenate(gated, axis=0)
    sums = jnp.sum(gated * gated, axis=1, keepdims=True)
    sum_row = jnp.sum(jnp.where(eye, sums, 0.0), axis=0, keepdims=True)
    ss_l[tok] = jnp.broadcast_to(sum_row, (8, rows))
    for o in range(1, n_tok):
        ship(7, o, ss_l.at[tok], ss_l.at[tok])
        first[7, o] = started[-1]

    for s in range(seqs):
        x, dtx, run = saved[s]
        alive = iota((draft, width), 0) < acc_ref[s]
        end = -rate_x * jnp.sum(jnp.where(alive, dtx, 0.0), axis=0, keepdims=True)
        weight = jnp.where(alive, jnp.exp(jnp.where(alive, end - run, 0.0)) * dtx, 0.0)
        flow = b_l[s].astype(F32).T.astype(BF16)
        new = jnp.exp(end) * st_l[s].astype(F32) + dot(flow, (x * weight).astype(BF16))
        cm_s[s] = new.astype(BF16)

    for o in range(1, n_tok):
        first[7, o].wait_recv()
    totals = jnp.zeros((1, rows), F32)
    for t in range(n_tok):
        totals = totals + ss_l[t][0:1, :]
    col = jnp.sum(jnp.where(eye, totals, 0.0), axis=1, keepdims=True)
    held[12].wait()
    gain = gain_ref[:, place(tok, width)]
    normed = gated * lax.rsqrt(col / (width * n_tok) + EPSILON) * gain
    normed = dot(swap, normed.astype(BF16)).astype(BF16)

    held[7].wait()
    tile = min(512, span)
    rs = {}
    pairs = []
    half = group // 2
    side = lax.rem(tok, 2)
    lines = n_tok // 2
    slot = head * lines + tok // 2

    def forward(ch):
        pairs[ch].wait_recv()
        piece = pl.ds(ch * span, span)
        red[:, :, piece] = (
            part[side, :, :, piece].astype(F32) + pair_l[:, :, piece].astype(F32)
        ).astype(BF16)
        for o in range(1, half):
            peer = lax.rem(slot + o, half)
            copy = pltpu.make_async_remote_copy(
                src_ref=red.at[peer, :, piece], dst_ref=rs_l.at[o, :, piece],
                send_sem=rs_send.at[ch, o], recv_sem=rs_recv.at[ch, o],
                device_id={"head": peer // lines, "tok": lax.rem(peer, lines) * 2 + side},
                device_id_type=MESH,
            )
            copy.start()
            rs[ch, o] = copy

    for ch in range(chunks):
        for start in range(ch * span, (ch + 1) * span, tile):
            val = dot(normed, w_v[:, start : start + tile]).astype(BF16)
            for p in range(2):
                for g in range(half):
                    at = (p * half + g) * each
                    part[p, g, :, start : start + tile] = val[at : at + each]
        piece = pl.ds(ch * span, span)
        copy = pltpu.make_async_remote_copy(
            src_ref=part.at[1 - side, :, :, piece], dst_ref=pair_l.at[:, :, piece],
            send_sem=pair_send.at[ch], recv_sem=pair_recv.at[ch],
            device_id={"tok": tok + 1 - 2 * side}, device_id_type=MESH,
        )
        copy.start()
        pairs.append(copy)
        if ch > 0:
            forward(ch - 1)
    forward(chunks - 1)

    for o in range(1, n_tok):
        first[6, o].wait_recv()
    held[6].wait()
    held[8].wait()
    for copy in held[9:12]:
        copy.wait()
    scale = att ** (-0.5)
    m_rows = per_kv * draft
    big = iota((m_rows, m_rows), 0) == iota((m_rows, m_rows), 1)
    position = tok * cache + iota((1, cache), 1)
    draft_at = tok * block + iota((draft, block), 1)
    seen = draft_at <= iota((draft, block), 0)
    seen = jnp.concatenate([seen.astype(F32)] * per_kv, axis=0) > 0.5
    for s in range(seqs):
        q = jnp.concatenate([q_l[s, :, h * att : (h + 1) * att] for h in range(per_kv)], axis=0)
        old = lax.dot_general(q, k_v[s], NT, preferred_element_type=F32)
        old = jnp.where(position < len_ref[s], old, MASKED)
        new = lax.dot_general(q, dk_ref[s], NT, preferred_element_type=F32)
        new = jnp.where(seen, new, MASKED)
        peak = jnp.maximum(
            jnp.max(old, axis=1, keepdims=True), jnp.max(new, axis=1, keepdims=True)
        )
        peak = jnp.maximum(peak, FLOOR)
        old = jnp.exp((old - peak) * scale)
        new = jnp.exp((new - peak) * scale)
        total = jnp.sum(old, axis=1, keepdims=True) + jnp.sum(new, axis=1, keepdims=True)
        numer = dot(old.astype(BF16), v_v[s]) + dot(new.astype(BF16), dv_ref[s])
        safe = jnp.maximum(total, 1e-30)
        ctx = (numer / safe).astype(BF16)
        level = jnp.where(total > 0.0, peak * scale + jnp.log(safe), MASKED)
        for h in range(per_kv):
            n_s[s, h] = ctx[h * draft : (h + 1) * draft]
        stat_l[tok, s : s + 1, :] = jnp.sum(jnp.where(big, level, 0.0), axis=0, keepdims=True)
    for o in range(1, n_tok):
        to = lax.rem(tok + o, n_tok)
        ship(8, o, stat_l.at[tok], stat_l.at[tok])
        first[8, o] = started[-1]
        ship(9, o, n_s.at[:, :, place(to, block), :], n_l.at[tok])
        first[9, o] = started[-1]
    for o in range(1, n_tok):
        to = lax.rem(tok + o, n_tok)
        ship(10, o, cm_s.at[:, place(to, cols), :], cm_l.at[:, :, place(tok, width)])
        first[10, o] = started[-1]
    n_l[tok] = n_s[:, :, mine, :]
    cm_l[:, :, place(tok, width)] = cm_s[:, place(tok, cols), :]

    for ch in range(chunks):
        for o in range(1, half):
            rs[ch, o].wait_recv()
        for start in range(ch * span, (ch + 1) * span, tile):
            acc = red[slot, :, start : start + tile].astype(F32)
            for o in range(1, half):
                acc = acc + rs_l[o, :, start : start + tile].astype(F32)
            out_ref[:, start : start + tile] = acc.astype(BF16)

    for o in range(1, n_tok):
        first[8, o].wait_recv()
        first[9, o].wait_recv()
    m_own = per_kv * block
    lanes = iota((m_own, m_rows), 1)
    r = iota((m_own, m_rows), 0)
    want = None
    for h in range(per_kv):
        t = r - h * block
        hit = (t >= 0) & (t < block) & (lanes == h * draft + tok * block + t)
        want = hit if want is None else want | hit
    for s in range(seqs):
        levels = [
            jnp.sum(jnp.where(want, stat_l[t][s : s + 1, :], 0.0), axis=1, keepdims=True)
            for t in range(n_tok)
        ]
        top = functools.reduce(jnp.maximum, levels)
        weights = [jnp.exp(level - top) for level in levels]
        den = functools.reduce(jnp.add, weights)
        acc = jnp.zeros((m_own, att), F32)
        for t in range(n_tok):
            got = jnp.concatenate([n_l[t, s, h].astype(F32) for h in range(per_kv)], axis=0)
            acc = acc + weights[t] * got
        acc = (acc / den).astype(BF16)
        for h in range(per_kv):
            ctx_ref[s, :, h * att : (h + 1) * att] = acc[h * block : (h + 1) * block]

    for o in range(1, n_tok):
        first[10, o].wait_recv()
    for s in range(seqs):
        for h in range(heads):
            com_ref[s, h] = cm_l[s, :, h * size : (h + 1) * size]
    for copy in started:
        copy.wait_send()
    for copy in pairs + list(rs.values()):
        copy.wait_send()


def body(
    mamba_input, gate_input, in_b, in_c, step_size, decay_rate, skip_weight, norm_gain,
    ssm_state, out_weight, queries, draft_token_keys, draft_values, cached_key_rows,
    cache_values, cache_len, accepted,
):
    n_tok = lax.axis_size("tok")
    n_head = lax.axis_size("head")
    group = n_head * n_tok
    seqs, block, features = mamba_input.shape
    heads = decay_rate.shape[0]
    size = features // heads
    cols = ssm_state.shape[3]
    state = cols * n_tok
    draft = block * n_tok
    width = features // n_tok
    att = draft_token_keys.shape[2]
    per_kv = queries.shape[2] // att
    cache = cached_key_rows.shape[1]
    out_cols = out_weight.shape[1]
    rows = seqs * draft
    each = rows // group
    chunks = 4
    half = group // 2
    turned = jnp.transpose(ssm_state, (0, 1, 3, 2))
    anys = [pl.BlockSpec(memory_space=pl.ANY)] * 13
    smems = [pl.BlockSpec(memory_space=pltpu.SMEM)] * 4
    out, ctx, com = pl.pallas_call(
        functools.partial(kernel, (n_head, n_tok, seqs, block, heads, chunks)),
        out_shape=(
            jax.ShapeDtypeStruct((each, out_cols), BF16),
            jax.ShapeDtypeStruct((seqs, block, per_kv * att), BF16),
            jax.ShapeDtypeStruct((seqs, heads, cols, size), BF16),
        ),
        in_specs=anys + smems,
        out_specs=[pl.BlockSpec(memory_space=pltpu.VMEM)] * 3,
        scratch_shapes=[
            pltpu.VMEM((seqs, draft, width), BF16),
            pltpu.VMEM((seqs, draft, width), BF16),
            pltpu.VMEM((seqs, draft, state), BF16),
            pltpu.VMEM((seqs, draft, state), BF16),
            pltpu.VMEM((seqs, draft, heads), BF16),
            pltpu.VMEM((seqs, state, width), BF16),
            pltpu.VMEM((seqs, draft, per_kv * att), BF16),
            pltpu.VMEM((seqs, cache, att), BF16),
            pltpu.VMEM((seqs, cache, att), BF16),
            pltpu.VMEM(out_weight.shape, BF16),
            pltpu.VMEM((n_tok, 8, rows), F32),
            pltpu.VMEM((seqs, state, width), BF16),
            pltpu.VMEM((seqs, cols, features), BF16),
            pltpu.VMEM((seqs, per_kv, draft, att), BF16),
            pltpu.VMEM((n_tok, seqs, per_kv, block, att), BF16),
            pltpu.VMEM((n_tok, seqs, per_kv * draft), F32),
            pltpu.VMEM((2, half, each, out_cols), BF16),
            pltpu.VMEM((half, each, out_cols), BF16),
            pltpu.VMEM((seqs, block, att), BF16),
            pltpu.VMEM((seqs, block, att), BF16),
            pltpu.VMEM((1, features), F32),
            pltpu.VMEM((seqs, heads, cols, size), BF16),
            pltpu.VMEM((seqs, cols, features), BF16),
            pltpu.VMEM((half, each, out_cols), BF16),
            pltpu.VMEM((half, each, out_cols), BF16),
            pltpu.SemaphoreType.DMA((11, n_tok)),
            pltpu.SemaphoreType.DMA((11, n_tok)),
            pltpu.SemaphoreType.DMA((chunks, half)),
            pltpu.SemaphoreType.DMA((chunks, half)),
            pltpu.SemaphoreType.DMA((chunks,)),
            pltpu.SemaphoreType.DMA((chunks,)),
            pltpu.SemaphoreType.DMA((13,)),
        ],
        compiler_params=pltpu.CompilerParams(
            collective_id=0, has_side_effects=True, vmem_limit_bytes=67043328
        ),
        name="hybrid",
    )(
        mamba_input, gate_input, in_b, in_c, step_size, turned, queries, cached_key_rows,
        cache_values, out_weight, draft_token_keys, draft_values,
        norm_gain.reshape(1, features), decay_rate, skip_weight, cache_len, accepted,
    )
    mamba_out = out.reshape(draft // group, seqs, out_cols)
    committed = jnp.transpose(com, (0, 1, 3, 2))
    return (mamba_out, ctx, committed)


def solution(mesh):
    in_specs = (
        P("dp", "tok", "head"),
        P("dp", "tok", "head"),
        P("dp", "tok", "head"),
        P("dp", "tok", "head"),
        P("dp", "tok", "head"),
        P("head"),
        P("head"),
        P("head"),
        P("dp", "head", None, "tok"),
        P(("head", "tok"), None),
        P("dp", "tok", "head"),
        P("dp", "tok", "head"),
        P("dp", "tok", "head"),
        P("dp", "tok", "head"),
        P("dp", "tok", "head"),
        P("dp"),
        P("dp"),
    )
    out_specs = (
        P(("head", "tok"), "dp", None),
        P("dp", "tok", "head"),
        P("dp", "head", None, "tok"),
    )
    return jax.shard_map(body, mesh=mesh, in_specs=in_specs, out_specs=out_specs, check_vma=False)
```

profile of v0, /device:TPU:0, one launch (start us, length us, event | category | flops | bytes accessed | tf_op | source)
XLA Modules:
  0.0 32.7 jit_solution(2454730275662589437)
XLA Ops:
  0.6 27.3 %hybrid.1 = (bf16[16,4096]{1,0:T(8,128)(2,1)}, bf16[2,16,512]{2,1,0:T(8,128)(2,1)}, bf16[2,16,32,64]{3,2,1,0:T(8,128)(2,1)}) custom-call(bf16[2,16,1024]{2,1,0:T(8,128)(2,1)} %x_in.1, bf16[2,16,1024]{2,1,0:T(8,128)(2,1)} %z_in.1, bf16[2,16,128]{2,1,0:T(8,128)(2,1)} %b_in.1, bf16[2,16,128]{2,1,0:T(8,128)(2,1)} %c_in.1, bf16[2,16,16]{2,1,0:T(8,128)(2,1)} %dt_in.1, ...), custom_call_target="tpu_custom_call" | custom-call | tf_op jit(solution)/shard_map/hybrid/pallas_call | solution.py:368
  28.0 1.7 %reshape.13 = bf16[8,2,4096]{2,1,0:T(2,128)(2,1)} reshape(bf16[16,4096]{1,0:T(8,128)(2,1)} %get-tuple-element.6) | data formatting | bytes 262144 | tf_op jit(solution)/shard_map/reshape | solution.py:420
  29.7 1.4 %copy.22 = bf16[2,16,512]{2,1,0:T(8,128)(2,1)} copy(bf16[2,16,512]{2,1,0:T(8,128)(2,1)} %get-tuple-element.13) | data formatting | bytes 65536
  31.0 1.7 %copy.23 = bf16[2,16,64,32]{2,3,1,0:T(8,128)(2,1)} copy(bf16[2,16,64,32]{2,3,1,0:T(8,128)(2,1)} %bitcast.3) | data formatting | bytes 262144
where the time goes:
time: 32.9 us; the launch traced here: 32.7 us
  Pallas kernels  27.3 us (83%)
  local copies, waits for them, and re-layouts  4.71 us (14%)
  between operations  0.65 us (2%)
    pallas_call x1, Pallas kernels, body(): pl.pallas_call(functools.partial(kernel, (n_head, n_tok, seqs, block, hea...  27.3 us
    unnamed x2, local copies, waits for them, and re-layouts  3.04 us
    reshape x1, local copies, waits for them, and re-layouts, body(): mamba_out = out.reshape(draft // group, seqs, out_cols)  1.67 us

commit v1 on v0

v1 whole, which is shorter than its diff:
```python
import functools
import jax
import jax.numpy as jnp
from jax import lax
from jax.experimental import pallas as pl
from jax.experimental.pallas import tpu as pltpu
from jax.sharding import PartitionSpec as P

EPSILON = 1e-05
MASKED = -1e30
FLOOR = -1e29
MESH = pl.DeviceIdType.MESH
F32 = jnp.float32
BF16 = jnp.bfloat16
NT = (((1,), (1,)), ((), ()))


def dot(a, b):
    return jnp.dot(a, b, preferred_element_type=F32)


def iota(shape, dim):
    return lax.broadcasted_iota(jnp.int32, shape, dim)


def kernel(
    dims,
    x_in, z_in, b_in, c_in, dt_in, st_in, q_in, k_in, v_in, w_in,
    dk_in, dv_in, gain_in, rate_in, skip_in, len_in, acc_in,
    out_ref, ctx_ref, com_ref,
    x_l, z_l, b_l, c_l, dt_l, st_l, q_l, k_v, v_v, w_v, x_v, z_v,
    ss_l, cm_s, cm_l, n_s, n_l, stat_l, part, rs_l,
    dk_ref, dv_ref, gain_ref, raw_v, turn_v, pair_l, red,
    rate_ref, skip_ref, len_ref, acc_ref,
    gat_send, gat_recv, send, recv, ss_send, ss_recv,
    rs_send, rs_recv, pair_send, pair_recv, local,
):
    n_head, n_tok, seqs, block, heads, chunks = dims
    group = n_head * n_tok
    tok = lax.axis_index("tok")
    head = lax.axis_index("head")
    me = head * n_tok + tok
    draft = block * n_tok
    width = x_l.shape[2]
    own = heads // n_tok
    size = width // own
    state = st_l.shape[1]
    cols = state // n_tok
    att = k_v.shape[2]
    per_kv = q_l.shape[2] // att
    cache = k_v.shape[1]
    rows = seqs * draft
    each = rows // group
    out_cols = w_v.shape[1]
    span = out_cols // chunks
    half = group // 2
    side = lax.rem(tok, 2)
    line = tok // 2
    lines = n_tok // 2
    slot = head * lines + line

    def place(index, unit):
        return pl.ds(pl.multiple_of(index * unit, unit), unit)

    barrier = pltpu.get_barrier_semaphore()
    for o in range(1, group):
        peer = lax.rem(me + o, group)
        pl.semaphore_signal(
            barrier, inc=1,
            device_id={"head": peer // n_tok, "tok": lax.rem(peer, n_tok)},
            device_id_type=MESH,
        )

    mine = place(tok, block)
    sources = {
        "st": (st_in, raw_v),
        "q": (q_in, q_l.at[:, mine, :]),
        "b": (b_in, b_l.at[:, mine, :]),
        "c": (c_in, c_l.at[:, mine, :]),
        "dt": (dt_in, dt_l.at[:, mine, :]),
        "x": (x_in, x_v),
        "z": (z_in, z_v),
        "k": (k_in, k_v),
        "v": (v_in, v_v),
        "dk": (dk_in, dk_ref),
        "dv": (dv_in, dv_ref),
        "len": (len_in, len_ref),
        "acc": (acc_in, acc_ref),
        "rate": (rate_in, rate_ref),
        "skip": (skip_in, skip_ref),
        "gain": (gain_in, gain_ref),
        "w": (w_in, w_v),
    }
    held = {}
    for i, (name, (src, dst)) in enumerate(sources.items()):
        held[name] = pltpu.make_async_copy(src, dst, local.at[i])
        held[name].start()

    held["st"].wait()
    for s in range(seqs):
        turn_v[s] = jnp.concatenate(
            [raw_v[s, h].astype(F32) for h in range(heads)], axis=1
        ).astype(BF16)
    st_l[:, place(tok, cols), :] = turn_v[:, :, place(tok, width)]
    for name in ("q", "b", "c", "dt", "x", "z"):
        held[name].wait()
    x_l[:, mine, :] = x_v[:, :, place(tok, width)]
    z_l[:, mine, :] = z_v[:, :, place(tok, width)]

    pl.semaphore_wait(barrier, group - 1)

    started = []

    def remote(src, dst, send_sem, recv_sem, device):
        copy = pltpu.make_async_remote_copy(
            src_ref=src, dst_ref=dst, send_sem=send_sem, recv_sem=recv_sem,
            device_id=device, device_id_type=MESH,
        )
        copy.start()
        started.append(copy)
        return copy

    partner = {"tok": tok + 1 - 2 * side}
    shared = (q_l, b_l, c_l, dt_l)
    gathered = {}

    def spread(kind, ref, index, at, device):
        part_at = ref.at[:, place(at, block), :]
        gathered[kind, index] = remote(
            part_at, part_at, gat_send.at[kind, index], gat_recv.at[kind, index], device
        )

    for o in range(1, lines):
        there = {"tok": lax.rem(line + o, lines) * 2 + side}
        for kind, ref in enumerate(shared):
            spread(kind, ref, o, tok, there)
    for kind, ref in enumerate(shared):
        spread(kind, ref, 0, tok, partner)

    first = {}

    def ship(kind, o, src, dst):
        first[kind, o] = remote(
            src, dst, send.at[kind, o], recv.at[kind, o], {"tok": lax.rem(tok + o, n_tok)}
        )

    for kind in range(3):
        for o in range(1, n_tok):
            to = lax.rem(tok + o, n_tok)
            src, dst = (
                (turn_v.at[:, :, place(to, width)], st_l.at[:, place(tok, cols), :]),
                (x_v.at[:, :, place(to, width)], x_l.at[:, mine, :]),
                (z_v.at[:, :, place(to, width)], z_l.at[:, mine, :]),
            )[kind]
            ship(kind, o, src, dst)

    for name in ("rate", "skip", "len", "acc"):
        held[name].wait()
    lane = iota((1, width), 1)
    rate_x = jnp.zeros((1, width), F32)
    skip_x = jnp.zeros((1, width), F32)
    for h in range(own):
        inside = (lane >= h * size) & (lane < (h + 1) * size)
        rate_x = jnp.where(inside, rate_ref[tok * own + h], rate_x)
        skip_x = jnp.where(inside, skip_ref[tok * own + h], skip_x)
    offset = iota((heads, width), 1) - (iota((heads, width), 0) - tok * own) * size
    pick = ((offset >= 0) & (offset < size)).astype(F32).astype(BF16)
    causal = iota((draft, draft), 0) >= iota((draft, draft), 1)
    lower = causal.astype(F32).astype(BF16)

    per = draft // group

    def targets(shape, dim):
        source = iota(shape, dim)
        target = jnp.zeros(shape, jnp.int32)
        for s in range(seqs):
            for g in range(group):
                start = s * draft + g * per
                base = (g % 2) * (rows // 2) + (g // 2) * each + s
                inside = (source >= start) & (source < start + per)
                target = jnp.where(inside, (source - start) * seqs + base, target)
        return target

    swap = (iota((rows, rows), 0) == targets((1, rows), 1)).astype(F32).astype(BF16)
    moved = targets((rows, 1), 0) == iota((rows, rows), 1)

    for o in range(1, lines):
        for kind, ref in enumerate(shared):
            gathered[kind, o].wait_recv()
            origin = lax.rem(line - o + lines, lines) * 2 + side
            spread(kind, ref, lines - 1 + o, origin, partner)
    gathered[0, 0].wait_recv()
    for o in range(1, lines):
        gathered[0, lines - 1 + o].wait_recv()
    for name in ("k", "v", "dk", "dv"):
        held[name].wait()
    scale = att ** (-0.5)
    m_rows = per_kv * draft
    big = iota((m_rows, m_rows), 0) == iota((m_rows, m_rows), 1)
    position = tok * cache + iota((1, cache), 1)
    draft_at = tok * block + iota((draft, block), 1)
    seen = draft_at <= iota((draft, block), 0)
    seen = jnp.concatenate([seen.astype(F32)] * per_kv, axis=0) > 0.5
    for s in range(seqs):
        q = jnp.concatenate([q_l[s, :, h * att : (h + 1) * att] for h in range(per_kv)], axis=0)
        old = lax.dot_general(q, k_v[s], NT, preferred_element_type=F32)
        old = jnp.where(position < len_ref[s], old, MASKED)
        new = lax.dot_general(q, dk_ref[s], NT, preferred_element_type=F32)
        new = jnp.where(seen, new, MASKED)
        peak = jnp.maximum(
            jnp.max(old, axis=1, keepdims=True), jnp.max(new, axis=1, keepdims=True)
        )
        peak = jnp.maximum(peak, FLOOR)
        old = jnp.exp((old - peak) * scale)
        new = jnp.exp((new - peak) * scale)
        total = jnp.sum(old, axis=1, keepdims=True) + jnp.sum(new, axis=1, keepdims=True)
        numer = dot(old.astype(BF16), v_v[s]) + dot(new.astype(BF16), dv_ref[s])
        safe = jnp.maximum(total, 1e-30)
        ctx = (numer / safe).astype(BF16)
        level = jnp.where(total > 0.0, peak * scale + jnp.log(safe), MASKED)
        for h in range(per_kv):
            n_s[s, h] = ctx[h * draft : (h + 1) * draft]
        stat_l[tok, s : s + 1, :] = jnp.sum(jnp.where(big, level, 0.0), axis=0, keepdims=True)
    for o in range(1, n_tok):
        to = lax.rem(tok + o, n_tok)
        ship(3, o, stat_l.at[tok], stat_l.at[tok])
        ship(4, o, n_s.at[:, :, place(to, block), :], n_l.at[tok])
    n_l[tok] = n_s[:, :, mine, :]

    for kind in range(1, len(shared)):
        for index in range(n_tok):
            if (kind, index) in gathered and not 1 <= index < lines:
                gathered[kind, index].wait_recv()
    for o in range(1, n_tok):
        first[0, o].wait_recv()
        first[1, o].wait_recv()
    saved = []
    for s in range(seqs):
        x = x_l[s].astype(F32)
        dtx = dot(dt_l[s], pick)
        run = -rate_x * dot(lower, dtx.astype(BF16))
        alive = iota((draft, width), 0) < acc_ref[s]
        end = -rate_x * jnp.sum(jnp.where(alive, dtx, 0.0), axis=0, keepdims=True)
        weight = jnp.where(alive, jnp.exp(jnp.where(alive, end - run, 0.0)) * dtx, 0.0)
        flow = b_l[s].astype(F32).T.astype(BF16)
        new = jnp.exp(end) * st_l[s].astype(F32) + dot(flow, (x * weight).astype(BF16))
        cm_s[s] = new.astype(BF16)
        saved.append((x, dtx, run))
    for o in range(1, n_tok):
        to = lax.rem(tok + o, n_tok)
        ship(5, o, cm_s.at[:, place(to, cols), :], cm_l.at[:, :, place(tok, width)])
    cm_l[:, :, place(tok, width)] = cm_s[:, place(tok, cols), :]

    for o in range(1, n_tok):
        first[2, o].wait_recv()
    held["gain"].wait()
    gated = []
    for s in range(seqs):
        x, dtx, run = saved[s]
        z = z_l[s].astype(F32)
        scaled = (x * dtx * jnp.exp(-run)).astype(BF16)
        mix = lax.dot_general(c_l[s], b_l[s], NT, preferred_element_type=F32)
        mix = jnp.where(causal, mix, 0.0).astype(BF16)
        y = jnp.exp(run) * (dot(mix, scaled) + dot(c_l[s], st_l[s])) + skip_x * x
        gated.append(y * z / (1.0 + jnp.exp(-z)))
    gated = jnp.concatenate(gated, axis=0)
    sums = jnp.sum(gated * gated, axis=1, keepdims=True)
    ss_l[me, 0:1, :] = jnp.sum(jnp.where(moved, sums, 0.0), axis=0, keepdims=True)
    squares = []
    for o in range(1, group):
        peer = lax.rem(me + o, group)
        squares.append(
            remote(
                ss_l.at[me], ss_l.at[me], ss_send.at[o], ss_recv.at[o],
                {"head": peer // n_tok, "tok": lax.rem(peer, n_tok)},
            )
        )
    gain = gain_ref[:, place(tok, width)]
    normed = dot(swap, (gated * gain).astype(BF16)).astype(BF16)

    held["w"].wait()
    tile = min(512, span)
    rs = {}
    pairs = []

    def forward(ch):
        pairs[ch].wait_recv()
        piece = pl.ds(ch * span, span)
        red[:, :, piece] = (
            part[side, :, :, piece].astype(F32) + pair_l[:, :, piece].astype(F32)
        ).astype(BF16)
        for o in range(1, half):
            peer = lax.rem(slot + o, half)
            rs[ch, o] = remote(
                red.at[peer, :, piece], rs_l.at[o, :, piece],
                rs_send.at[ch, o], rs_recv.at[ch, o],
                {"head": peer // lines, "tok": lax.rem(peer, lines) * 2 + side},
            )

    for ch in range(chunks):
        for start in range(ch * span, (ch + 1) * span, tile):
            val = dot(normed, w_v[:, start : start + tile]).astype(BF16)
            for p in range(2):
                for g in range(half):
                    at = (p * half + g) * each
                    part[p, g, :, start : start + tile] = val[at : at + each]
        piece = pl.ds(ch * span, span)
        pairs.append(
            remote(
                part.at[1 - side, :, :, piece], pair_l.at[:, :, piece],
                pair_send.at[ch], pair_recv.at[ch], partner,
            )
        )
        if ch > 0:
            forward(ch - 1)
    forward(chunks - 1)

    for o in range(1, n_tok):
        first[3, o].wait_recv()
        first[4, o].wait_recv()
    m_own = per_kv * block
    lanes = iota((m_own, m_rows), 1)
    r = iota((m_own, m_rows), 0)
    want = None
    for h in range(per_kv):
        t = r - h * block
        hit = (t >= 0) & (t < block) & (lanes == h * draft + tok * block + t)
        want = hit if want is None else want | hit
    for s in range(seqs):
        levels = [
            jnp.sum(jnp.where(want, stat_l[t][s : s + 1, :], 0.0), axis=1, keepdims=True)
            for t in range(n_tok)
        ]
        top = functools.reduce(jnp.maximum, levels)
        weights = [jnp.exp(level - top) for level in levels]
        den = functools.reduce(jnp.add, weights)
        acc = jnp.zeros((m_own, att), F32)
        for t in range(n_tok):
            got = jnp.concatenate([n_l[t, s, h].astype(F32) for h in range(per_kv)], axis=0)
            acc = acc + weights[t] * got
        acc = (acc / den).astype(BF16)
        for h in range(per_kv):
            ctx_ref[s, :, h * att : (h + 1) * att] = acc[h * block : (h + 1) * block]

    for o in range(1, n_tok):
        first[5, o].wait_recv()
    for s in range(seqs):
        for h in range(heads):
            com_ref[s, h] = cm_l[s, :, h * size : (h + 1) * size]

    for copy in squares:
        copy.wait_recv()
    base = side * (rows // 2) + slot * each
    here = iota((each, rows), 1) == base + iota((each, rows), 0)
    factors = []
    for o in range(half):
        origin = lax.rem(slot - o + half, half) // lines
        total = jnp.zeros((1, rows), F32)
        for t in range(n_tok):
            total = total + ss_l[origin * n_tok + t][0:1, :]
        column = jnp.sum(jnp.where(here, total, 0.0), axis=1, keepdims=True)
        factors.append(lax.rsqrt(column / (width * n_tok) + EPSILON))
    for ch in range(chunks):
        for o in range(1, half):
            rs[ch, o].wait_recv()
        for start in range(ch * span, (ch + 1) * span, tile):
            acc = red[slot, :, start : start + tile].astype(F32) * factors[0]
            for o in range(1, half):
                acc = acc + rs_l[o, :, start : start + tile].astype(F32) * factors[o]
            acc = acc.astype(BF16)
            for d in range(each // seqs):
                out_ref[d, :, start : start + tile] = acc[d * seqs : (d + 1) * seqs]

    for copy in started:
        copy.wait_send()


def finish(out_v, ctx_v, com_v, out_ref, ctx_ref, com_ref, sems):
    copies = [
        pltpu.make_async_copy(src, dst, sems.at[i])
        for i, (src, dst) in enumerate(((out_v, out_ref), (com_v, com_ref), (ctx_v, ctx_ref)))
    ]
    for copy in copies:
        copy.start()
    for copy in copies:
        copy.wait()


def body(
    mamba_input, gate_input, in_b, in_c, step_size, decay_rate, skip_weight, norm_gain,
    ssm_state, out_weight, queries, draft_token_keys, draft_values, cached_key_rows,
    cache_values, cache_len, accepted,
):
    n_tok = lax.axis_size("tok")
    n_head = lax.axis_size("head")
    group = n_head * n_tok
    seqs, block, features = mamba_input.shape
    heads = decay_rate.shape[0]
    size = features // heads
    cols = ssm_state.shape[3]
    state = cols * n_tok
    draft = block * n_tok
    width = features // n_tok
    att = draft_token_keys.shape[2]
    per_kv = queries.shape[2] // att
    cache = cached_key_rows.shape[1]
    out_cols = out_weight.shape[1]
    rows = seqs * draft
    each = rows // group
    chunks = 4
    half = group // 2
    turned = jnp.transpose(ssm_state, (0, 1, 3, 2))
    shapes = (
        (each // seqs, seqs, out_cols),
        (seqs, block, per_kv * att),
        (seqs, heads, cols, size),
    )
    operands = (
        mamba_input, gate_input, in_b, in_c, step_size, turned, queries, cached_key_rows,
        cache_values, out_weight, draft_token_keys, draft_values,
        norm_gain.reshape(1, features), decay_rate, skip_weight, cache_len, accepted,
    )
    vmem = pl.BlockSpec(memory_space=pltpu.VMEM)
    held = pl.pallas_call(
        functools.partial(kernel, (n_head, n_tok, seqs, block, heads, chunks)),
        out_shape=[pltpu.VMEM(shape, BF16) for shape in shapes],
        in_specs=[pl.BlockSpec(memory_space=pltpu.HBM)] * 17,
        out_specs=[vmem] * 3,
        scratch_shapes=[
            pltpu.VMEM((seqs, draft, width), BF16),
            pltpu.VMEM((seqs, draft, width), BF16),
            pltpu.VMEM((seqs, draft, state), BF16),
            pltpu.VMEM((seqs, draft, state), BF16),
            pltpu.VMEM((seqs, draft, heads), BF16),
            pltpu.VMEM((seqs, state, width), BF16),
            pltpu.VMEM((seqs, draft, per_kv * att), BF16),
            pltpu.VMEM((seqs, cache, att), BF16),
            pltpu.VMEM((seqs, cache, att), BF16),
            pltpu.VMEM(out_weight.shape, BF16),
            pltpu.VMEM((seqs, block, features), BF16),
            pltpu.VMEM((seqs, block, features), BF16),
            pltpu.VMEM((group, 1, rows), F32),
            pltpu.VMEM((seqs, state, width), BF16),
            pltpu.VMEM((seqs, cols, features), BF16),
            pltpu.VMEM((seqs, per_kv, draft, att), BF16),
            pltpu.VMEM((n_tok, seqs, per_kv, block, att), BF16),
            pltpu.VMEM((n_tok, seqs, per_kv * draft), F32),
            pltpu.VMEM((2, half, each, out_cols), BF16),
            pltpu.VMEM((half, each, out_cols), BF16),
            pltpu.VMEM((seqs, block, att), BF16),
            pltpu.VMEM((seqs, block, att), BF16),
            pltpu.VMEM((1, features), F32),
            pltpu.VMEM((seqs, heads, cols, size), BF16),
            pltpu.VMEM((seqs, cols, features), BF16),
            pltpu.VMEM((half, each, out_cols), BF16),
            pltpu.VMEM((half, each, out_cols), BF16),
            pltpu.SMEM(decay_rate.shape, F32),
            pltpu.SMEM(skip_weight.shape, F32),
            pltpu.SMEM(cache_len.shape, jnp.int32),
            pltpu.SMEM(accepted.shape, jnp.int32),
            pltpu.SemaphoreType.DMA((4, n_tok)),
            pltpu.SemaphoreType.DMA((4, n_tok)),
            pltpu.SemaphoreType.DMA((6, n_tok)),
            pltpu.SemaphoreType.DMA((6, n_tok)),
            pltpu.SemaphoreType.DMA((group,)),
            pltpu.SemaphoreType.DMA((group,)),
            pltpu.SemaphoreType.DMA((chunks, half)),
            pltpu.SemaphoreType.DMA((chunks, half)),
            pltpu.SemaphoreType.DMA((chunks,)),
            pltpu.SemaphoreType.DMA((chunks,)),
            pltpu.SemaphoreType.DMA((17,)),
        ],
        compiler_params=pltpu.CompilerParams(
            collective_id=0, has_side_effects=True, vmem_limit_bytes=40 * 1024 * 1024
        ),
        name="hybrid",
    )(*[pltpu.with_memory_space_constraint(a, pltpu.HBM) for a in operands])
    out, ctx, com = pl.pallas_call(
        finish,
        out_shape=[jax.ShapeDtypeStruct(shape, BF16) for shape in shapes],
        in_specs=[vmem] * 3,
        out_specs=[pl.BlockSpec(memory_space=pl.ANY)] * 3,
        scratch_shapes=[pltpu.SemaphoreType.DMA((3,))],
        compiler_params=pltpu.CompilerParams(vmem_limit_bytes=4 * 1024 * 1024),
        name="finish",
    )(*[pltpu.with_memory_space_constraint(a, pltpu.VMEM) for a in held])
    return (out, ctx, jnp.transpose(com, (0, 1, 3, 2)))


def solution(mesh):
    in_specs = (
        P("dp", "tok", "head"),
        P("dp", "tok", "head"),
        P("dp", "tok", "head"),
        P("dp", "tok", "head"),
        P("dp", "tok", "head"),
        P("head"),
        P("head"),
        P("head"),
        P("dp", "head", None, "tok"),
        P(("head", "tok"), None),
        P("dp", "tok", "head"),
        P("dp", "tok", "head"),
        P("dp", "tok", "head"),
        P("dp", "tok", "head"),
        P("dp", "tok", "head"),
        P("dp"),
        P("dp"),
    )
    out_specs = (
        P(("head", "tok"), "dp", None),
        P("dp", "tok", "head"),
        P("dp", "head", None, "tok"),
    )
    return jax.shard_map(body, mesh=mesh, in_specs=in_specs, out_specs=out_specs, check_vma=False)
```

time: 32.9 us -> 23.4 us (0.71)
  local copies, waits for them, and re-layouts: 4.71 us -> 0 us
  Pallas kernels: 27.3 us -> 22.6 us
    pallas_call x1, Pallas kernels: 27.3 us -> 21.8 us  [body(): pl.pallas_call(functools.partial(kernel, (n_head, n_tok, seqs, block, hea...]
    unnamed x2 -> x0, local copies, waits for them, and re-layouts: 3.04 us -> none
    reshape x1 -> x0, local copies, waits for them, and re-layouts: 1.67 us -> none  [body(): mamba_out = out.reshape(draft // group, seqs, out_cols)]
    pallas_call x0 -> x1, Pallas kernels: none -> 0.78 us  [body(): pl.pallas_call(finish, out_shape=[jax.ShapeDtypeStruct(shape, BF16) for s...]
where the time goes in v1:
time: 23.4 us; the launch traced here: 23.2 us
  Pallas kernels  22.6 us (97%)
  between operations  0.65 us (3%)
    pallas_call x1, Pallas kernels, body(): pl.pallas_call(functools.partial(kernel, (n_head, n_tok, seqs, block, hea...  21.8 us
    pallas_call x1, Pallas kernels, body(): pl.pallas_call(finish, out_shape=[jax.ShapeDtypeStruct(shape, BF16) for s...  0.78 us

profile of v1, /device:TPU:0, one launch (start us, length us, event | category | flops | bytes accessed | tf_op | source)
XLA Modules:
  0.0 23.2 jit_solution(1758402468264797146)
XLA Ops:
  0.6 21.8 %hybrid.1 = (bf16[8,2,4096]{2,1,0:T(2,128)(2,1)S(1)}, bf16[2,16,512]{2,1,0:T(8,128)(2,1)S(1)}, bf16[2,16,32,64]{3,2,1,0:T(8,128)(2,1)S(1)}) custom-call(bf16[2,16,1024]{2,1,0:T(8,128)(2,1)} %x_in.1, bf16[2,16,1024]{2,1,0:T(8,128)(2,1)} %z_in.1, bf16[2,16,128]{2,1,0:T(8,128)(2,1)} %b_in.1, bf16[2,16,128]{2,1,0:T(8,128)(2,1)} %c_in.1, ...), custom_call_target="tpu_custom_call" | custom-call | tf_op jit(solution)/shard_map/hybrid/pallas_call | solution.py:424
  22.4 0.8 %finish.1 = (bf16[8,2,4096]{2,1,0:T(2,128)(2,1)}, bf16[2,16,512]{2,1,0:T(8,128)(2,1)}, bf16[2,16,32,64]{3,2,1,0:T(8,128)(2,1)}) custom-call(bf16[8,2,4096]{2,1,0:T(2,128)(2,1)S(1)} %get-tuple-element.9.out_v, bf16[2,16,512]{2,1,0:T(8,128)(2,1)S(1)} %get-tuple-element.10.ctx_v, bf16[2,16,32,64]{3,2,1,0:T(8,128)(2,1)S(1)} %get-tuple-element.11.com_v), custom_call_target="tpu_custom_call" | custom-call | tf_op jit(solution)/shard_map/finish/pallas_call | solution.py:478

commit v2 on v1

v2 whole, which is shorter than its diff:
```python
import functools
import jax
import jax.numpy as jnp
from jax import lax
from jax.experimental import pallas as pl
from jax.experimental.pallas import tpu as pltpu
from jax.sharding import PartitionSpec as P

EPSILON = 1e-05
MASKED = -1e30
FLOOR = -1e29
MESH = pl.DeviceIdType.MESH
F32 = jnp.float32
BF16 = jnp.bfloat16
NT = (((1,), (1,)), ((), ()))


def dot(a, b):
    return jnp.dot(a, b, preferred_element_type=F32)


def iota(shape, dim):
    return lax.broadcasted_iota(jnp.int32, shape, dim)


def kernel(
    dims,
    x_in, z_in, b_in, c_in, dt_in, st_in, q_in, k_in, v_in, w_in,
    dk_in, dv_in, gain_in, rate_in, skip_in, len_in, acc_in,
    out_ref, ctx_ref, com_ref,
    xz_v, xz_l, bc_l, dt_l, raw_v, turn_v, st_l, q_l, kv_v, new_v, w_v, gain_v,
    ss_l, cm_s, cm_l, n_s, n_l, stat_s, stat_l,
    part, pair_l, red, one_a, one_b, mid_a, mid_b, two_a, two_b,
    rate_ref, skip_ref, len_ref, acc_ref,
    sent, q_recv, bc_recv, dt_recv, st_recv, xz_recv, got, ss_recv,
    pair_recv, one_recv, two_recv, local,
):
    n_head, n_tok, seqs, block, heads, chunks = dims
    group = n_head * n_tok
    tok = lax.axis_index("tok")
    head = lax.axis_index("head")
    me = head * n_tok + tok
    draft = block * n_tok
    width = xz_l.shape[3]
    own = heads // n_tok
    size = width // own
    state = st_l.shape[1]
    cols = state // n_tok
    att = kv_v.shape[3]
    per_kv = q_l.shape[2] // att
    cache = kv_v.shape[2]
    per = draft // group
    out_cols = w_v.shape[1]
    span = out_cols // chunks
    half = group // 2
    side = lax.rem(tok, 2)
    line = tok // 2
    lines = n_tok // 2
    slot = head * lines + line

    def place(index, unit):
        return pl.ds(pl.multiple_of(index * unit, unit), unit)

    barrier = pltpu.get_barrier_semaphore()
    for o in range(1, group):
        peer = lax.rem(me + o, group)
        pl.semaphore_signal(
            barrier, inc=1,
            device_id={"head": peer // n_tok, "tok": lax.rem(peer, n_tok)},
            device_id_type=MESH,
        )

    def take(sem, ref):
        pltpu.make_async_copy(ref, ref, sem).wait()

    mine = place(tok, block)
    for sem, src, dst in (
        (0, st_in, raw_v),
        (1, q_in, q_l.at[:, mine, :]),
        (2, b_in, bc_l.at[0, :, mine, :]),
        (2, c_in, bc_l.at[1, :, mine, :]),
        (3, dt_in, dt_l.at[:, mine, :]),
        (4, x_in, xz_v.at[:, 0]),
        (4, z_in, xz_v.at[:, 1]),
        (5, dk_in, new_v.at[0]),
        (5, dv_in, new_v.at[1]),
        (6, k_in, kv_v.at[0]),
        (6, v_in, kv_v.at[1]),
        (7, len_in, len_ref),
        (8, acc_in, acc_ref),
        (9, rate_in, rate_ref),
        (10, skip_in, skip_ref),
        (11, gain_in, gain_v),
        (12, w_in, w_v),
    ):
        pltpu.make_async_copy(src, dst, local.at[sem]).start()

    take(local.at[0], raw_v)
    for s in range(seqs):
        turn_v[s] = jnp.concatenate(
            [raw_v[s, h].astype(F32) for h in range(heads)], axis=1
        ).astype(BF16)
    st_l[:, place(tok, cols), :] = turn_v[:, :, place(tok, width)]
    take(local.at[1], q_l.at[:, mine, :])
    take(local.at[2], bc_l.at[:, :, mine, :])
    take(local.at[3], dt_l.at[:, mine, :])
    take(local.at[4], xz_v)
    xz_l[:, :, mine, :] = xz_v[:, :, :, place(tok, width)]

    pl.semaphore_wait(barrier, group - 1)

    def remote(kind, src, dst, recv_sem, device):
        pltpu.make_async_remote_copy(
            src_ref=src, dst_ref=dst, send_sem=sent.at[kind], recv_sem=recv_sem,
            device_id=device, device_id_type=MESH,
        ).start()

    flip = tok + 1 - 2 * side
    partner = {"tok": flip}

    def share(at, device, q_sem, sem, only=None):
        span_at = place(at, block)
        for kind, ref, recv in (
            (0, q_l.at[:, span_at, :], q_recv.at[q_sem]),
            (1, bc_l.at[:, :, span_at, :], bc_recv.at[sem]),
            (2, dt_l.at[:, span_at, :], dt_recv.at[sem]),
        ):
            if only is None or kind in only:
                remote(kind, ref, ref, recv, device)

    for o in range(1, lines):
        share(tok, {"tok": lax.rem(line + o, lines) * 2 + side}, o, o)
    share(tok, partner, 0, 0)
    for s in range(seqs):
        for o in range(1, n_tok):
            to = lax.rem(tok + o, n_tok)
            remote(
                3, turn_v.at[s, :, place(to, width)], st_l.at[s, place(tok, cols), :],
                st_recv.at[s], {"tok": to},
            )
        for o in range(1, n_tok):
            to = lax.rem(tok + o, n_tok)
            remote(
                4, xz_v.at[s, :, :, place(to, width)], xz_l.at[s, :, mine, :],
                xz_recv.at[s], {"tok": to},
            )

    for i, ref in ((7, len_ref), (8, acc_ref), (9, rate_ref), (10, skip_ref)):
        take(local.at[i], ref)
    take(local.at[5], new_v)
    take(local.at[6], kv_v)
    scale = att ** (-0.5)
    m_own = per_kv * block
    eye = iota((m_own, m_own), 0) == iota((m_own, m_own), 1)
    position = tok * cache + iota((1, cache), 1)
    inner = iota((block, block), 1) - iota((block, block), 0)
    inner = jnp.concatenate([inner] * per_kv, axis=0)

    def attend(t, n_to, stat_to):
        for s in range(seqs):
            q = jnp.concatenate(
                [q_l[s, place(t, block), h * att : (h + 1) * att] for h in range(per_kv)], axis=0
            )
            old = lax.dot_general(q, kv_v[0, s], NT, preferred_element_type=F32)
            old = jnp.where(position < len_ref[s], old, MASKED)
            new = lax.dot_general(q, new_v[0, s], NT, preferred_element_type=F32)
            new = jnp.where(inner <= (t - tok) * block, new, MASKED)
            peak = jnp.maximum(
                jnp.max(old, axis=1, keepdims=True), jnp.max(new, axis=1, keepdims=True)
            )
            peak = jnp.maximum(peak, FLOOR)
            old = jnp.exp((old - peak) * scale)
            new = jnp.exp((new - peak) * scale)
            total = jnp.sum(old, axis=1, keepdims=True) + jnp.sum(new, axis=1, keepdims=True)
            numer = dot(old.astype(BF16), kv_v[1, s]) + dot(new.astype(BF16), new_v[1, s])
            safe = jnp.maximum(total, 1e-30)
            level = jnp.where(total > 0.0, peak * scale + jnp.log(safe), MASKED)
            n_to[s] = (numer / safe).astype(BF16)
            stat_to[s : s + 1, :] = jnp.sum(jnp.where(eye, level, 0.0), axis=0, keepdims=True)

    def attend_for(t, index):
        attend(t, n_s.at[index], stat_s.at[index])
        remote(5, n_s.at[index], n_l.at[tok], got.at[0], {"tok": t})
        remote(6, stat_s.at[index], stat_l.at[tok], got.at[1], {"tok": t})

    attend(tok, n_l.at[tok], stat_l.at[tok])
    take(q_recv.at[0], q_l.at[:, mine, :])
    attend_for(flip, 0)
    for o in range(1, lines):
        origin = lax.rem(line - o + lines, lines) * 2 + side
        take(q_recv.at[o], q_l.at[:, mine, :])
        share(origin, partner, lines - 1 + o, 0, (0,))
    for o in range(1, lines):
        origin = lax.rem(line - o + lines, lines) * 2 + side
        take(bc_recv.at[o], bc_l.at[:, :, mine, :])
        take(dt_recv.at[o], dt_l.at[:, mine, :])
        share(origin, partner, 0, 0, (1, 2))
    for o in range(1, lines):
        attend_for(lax.rem(line - o + lines, lines) * 2 + side, o)
    for o in range(1, lines):
        take(q_recv.at[lines - 1 + o], q_l.at[:, mine, :])
        attend_for(lax.rem(line - o + lines, lines) * 2 + 1 - side, lines - 1 + o)

    lane = iota((1, width), 1)
    rate_x = jnp.zeros((1, width), F32)
    skip_x = jnp.zeros((1, width), F32)
    for h in range(own):
        inside = (lane >= h * size) & (lane < (h + 1) * size)
        rate_x = jnp.where(inside, rate_ref[tok * own + h], rate_x)
        skip_x = jnp.where(inside, skip_ref[tok * own + h], skip_x)
    offset = iota((heads, width), 1) - (iota((heads, width), 0) - tok * own) * size
    pick = ((offset >= 0) & (offset < size)).astype(F32).astype(BF16)
    causal = iota((draft, draft), 0) >= iota((draft, draft), 1)
    lower = causal.astype(F32).astype(BF16)

    def target(dim):
        source = iota((draft, draft), dim)
        result = jnp.zeros((draft, draft), jnp.int32)
        for g in range(group):
            base = (g % 2) * (draft // 2) + (g // 2) * per
            inside = (source >= g * per) & (source < (g + 1) * per)
            result = jnp.where(inside, source - g * per + base, result)
        return result

    swap = (iota((draft, draft), 0) == target(1)).astype(F32).astype(BF16)
    moved = target(0) == iota((draft, draft), 1)
    take(local.at[11], gain_v)
    gain = gain_v[:, place(tok, width)]
    take(local.at[12], w_v)
    take(bc_recv.at[0], bc_l.at[:, :, pl.ds(0, lines * block), :])
    take(dt_recv.at[0], dt_l.at[:, pl.ds(0, lines * block), :])

    tile = min(512, span)

    def piece_of(ch):
        return pl.ds(ch * span, span)

    def mix_tokens(s):
        x = xz_l[s, 0].astype(F32)
        z = xz_l[s, 1].astype(F32)
        dtx = dot(dt_l[s], pick)
        run = -rate_x * dot(lower, dtx.astype(BF16))
        scaled = (x * dtx * jnp.exp(-run)).astype(BF16)
        mix = lax.dot_general(bc_l[1, s], bc_l[0, s], NT, preferred_element_type=F32)
        mix = jnp.where(causal, mix, 0.0).astype(BF16)
        y = jnp.exp(run) * (dot(mix, scaled) + dot(bc_l[1, s], st_l[s])) + skip_x * x
        gated = y * z / (1.0 + jnp.exp(-z))
        sums = jnp.sum(gated * gated, axis=1, keepdims=True)
        ss_l[s, me] = jnp.sum(jnp.where(moved, sums, 0.0), axis=0, keepdims=True)
        for o in range(1, group):
            peer = lax.rem(me + o, group)
            remote(
                7, ss_l.at[s, me], ss_l.at[s, me], ss_recv.at[s],
                {"head": peer // n_tok, "tok": lax.rem(peer, n_tok)},
            )
        return dot(swap, (gated * gain).astype(BF16)).astype(BF16), (x, dtx, run)

    def project(s, normed):
        for ch in range(chunks):
            for start in range(ch * span, (ch + 1) * span, tile):
                val = dot(normed, w_v[:, start : start + tile])
                for p in range(2):
                    for g in range(half):
                        at = (p * half + g) * per
                        part[s, p, g // lines, g % lines, :, start : start + tile] = val[
                            at : at + per
                        ].astype(BF16)
            remote(
                8, part.at[s, 1 - side, :, :, :, piece_of(ch)],
                pair_l.at[s, :, :, :, piece_of(ch)], pair_recv.at[s, ch], partner,
            )

    def commit(s, saved):
        x, dtx, run = saved
        alive = iota((draft, width), 0) < acc_ref[s]
        end = -rate_x * jnp.sum(jnp.where(alive, dtx, 0.0), axis=0, keepdims=True)
        weight = jnp.where(alive, jnp.exp(jnp.where(alive, end - run, 0.0)) * dtx, 0.0)
        flow = bc_l[0, s].astype(F32).T.astype(BF16)
        new = jnp.exp(end) * st_l[s].astype(F32) + dot(flow, (x * weight).astype(BF16))
        cm_s[s] = new.astype(BF16)
        for o in range(1, n_tok):
            to = lax.rem(tok + o, n_tok)
            remote(
                9, cm_s.at[s, place(to, cols), :], cm_l.at[s, :, place(tok, width)],
                got.at[2], {"tok": to},
            )
        cm_l[s, :, place(tok, width)] = cm_s[s, place(tok, cols), :]

    def line_first(ch):
        return ch % 2 == 0

    def forward(s, ch):
        piece = piece_of(ch)
        take(pair_recv.at[s, ch], pair_l.at[s, :, :, :, piece])
        red[s, :, :, :, piece] = (
            part[s, side, :, :, :, piece].astype(F32) + pair_l[s, :, :, :, piece].astype(F32)
        ).astype(BF16)
        if line_first(ch):
            for o in range(1, lines):
                to = lax.rem(line + o, lines)
                remote(
                    10, red.at[s, :, to, :, piece], one_a.at[s, o, :, :, piece],
                    one_recv.at[s, ch, o - 1], {"tok": to * 2 + side},
                )
        else:
            for o in range(1, n_head):
                to = lax.rem(head + o, n_head)
                remote(
                    11, red.at[s, to, :, :, piece], one_b.at[s, o, :, :, piece],
                    one_recv.at[s, ch, o - 1], {"head": to},
                )

    def factor(s, origin, base, count):
        total = jnp.zeros((1, draft), F32)
        for t in range(n_tok):
            total = total + ss_l[s, origin * n_tok + t]
        here = iota((count, draft), 1) == base + iota((count, draft), 0)
        column = jnp.sum(jnp.where(here, total, 0.0), axis=1, keepdims=True)
        return lax.rsqrt(column / (width * n_tok) + EPSILON)

    def second(s, ch, factors):
        piece = piece_of(ch)
        if line_first(ch):
            for o in range(1, lines):
                take(one_recv.at[s, ch, o - 1], one_a.at[s, o, :, :, piece])
            total = red[s, :, line, :, piece].astype(F32)
            for o in range(1, lines):
                total = total + one_a[s, o, :, :, piece].astype(F32)
            mid_a[s, :, :, piece] = total.astype(BF16)
            for o in range(1, n_head):
                to = lax.rem(head + o, n_head)
                remote(
                    12, mid_a.at[s, to, :, piece], two_a.at[s, o, :, piece],
                    two_recv.at[s, ch, o - 1], {"head": to},
                )
        else:
            for o in range(1, n_head):
                take(one_recv.at[s, ch, o - 1], one_b.at[s, o, :, :, piece])
            for l in range(lines):
                near = slice(l * per, (l + 1) * per)
                total = red[s, head, l, :, piece].astype(F32) * factors[0][near]
                for o in range(1, n_head):
                    total = total + one_b[s, o, l, :, piece].astype(F32) * factors[o][near]
                mid_b[s, l, :, piece] = total.astype(BF16)
            for o in range(1, lines):
                to = lax.rem(line + o, lines)
                remote(
                    13, mid_b.at[s, to, :, piece], two_b.at[s, o, :, piece],
                    two_recv.at[s, ch, o - 1], {"tok": to * 2 + side},
                )

    def final(s, ch, factors):
        piece = piece_of(ch)
        if line_first(ch):
            for o in range(1, n_head):
                take(two_recv.at[s, ch, o - 1], two_a.at[s, o, :, piece])
            total = mid_a[s, head, :, piece].astype(F32) * factors[0]
            for o in range(1, n_head):
                total = total + two_a[s, o, :, piece].astype(F32) * factors[o]
        else:
            for o in range(1, lines):
                take(two_recv.at[s, ch, o - 1], two_b.at[s, o, :, piece])
            total = mid_b[s, line, :, piece].astype(F32)
            for o in range(1, lines):
                total = total + two_b[s, o, :, piece].astype(F32)
        return total

    for s in range(seqs):
        take(st_recv.at[s], st_l.at[s, pl.ds(0, (n_tok - 1) * cols), :])
        take(xz_recv.at[s], xz_l.at[s, :, pl.ds(0, (n_tok - 1) * block), :])
        normed, saved = mix_tokens(s)
        project(s, normed)
        commit(s, saved)
        for ch in range(chunks):
            forward(s, ch)

    take(got.at[0], n_l.at[pl.ds(0, n_tok - 1)])
    take(got.at[1], stat_l.at[pl.ds(0, n_tok - 1)])
    for s in range(seqs):
        levels = [
            jnp.sum(jnp.where(eye, stat_l[t, s : s + 1, :], 0.0), axis=1, keepdims=True)
            for t in range(n_tok)
        ]
        top = functools.reduce(jnp.maximum, levels)
        weights = [jnp.exp(level - top) for level in levels]
        den = functools.reduce(jnp.add, weights)
        acc = jnp.zeros((m_own, att), F32)
        for t in range(n_tok):
            acc = acc + weights[t] * n_l[t, s].astype(F32)
        acc = (acc / den).astype(BF16)
        for h in range(per_kv):
            ctx_ref[s, :, h * att : (h + 1) * att] = acc[h * block : (h + 1) * block]

    ours = side * (draft // 2) + head * lines * per
    narrow = []
    for s in range(seqs):
        take(ss_recv.at[s], ss_l.at[s, pl.ds(0, group - 1)])
        origins = [lax.rem(head - o + n_head, n_head) for o in range(n_head)]
        wide = [factor(s, origin, ours, lines * per) for origin in origins]
        narrow.append([factor(s, origin, ours + line * per, per) for origin in origins])
        for ch in range(chunks):
            second(s, ch, wide)

    take(got.at[2], cm_l.at[:, :, pl.ds(0, (n_tok - 1) * width)])
    for s in range(seqs):
        for h in range(heads):
            com_ref[s, h] = cm_l[s, :, h * size : (h + 1) * size]

    at, of = iota((per * seqs, per * seqs), 0), iota((per * seqs, per * seqs), 1)
    weave = jnp.zeros((per * seqs, per * seqs), F32)
    for s in range(seqs):
        weave = jnp.where(at == (of - s * per) * seqs + s, jnp.where((of >= s * per) & (of < (s + 1) * per), 1.0, weave), weave)
    weave = weave.astype(BF16)
    for ch in range(chunks):
        both = jnp.concatenate([final(s, ch, narrow[s]) for s in range(seqs)], axis=0)
        both = dot(weave, both.astype(BF16)).astype(BF16)
        for d in range(per):
            out_ref[d, :, piece_of(ch)] = both[d * seqs : (d + 1) * seqs]

    others = pl.ds(0, n_tok - 1)
    most = pl.ds(0, (n_tok - 1) * block)
    take(sent.at[0], q_l.at[:, most, :])
    take(sent.at[1], bc_l.at[:, :, most, :])
    take(sent.at[2], dt_l.at[:, most, :])
    take(sent.at[3], turn_v.at[:, :, pl.ds(0, (n_tok - 1) * width)])
    take(sent.at[4], xz_v.at[:, :, :, pl.ds(0, (n_tok - 1) * width)])
    take(sent.at[5], n_s.at[others])
    take(sent.at[6], stat_s.at[others])
    take(sent.at[7], ss_l.at[:, pl.ds(0, group - 1)])
    take(sent.at[8], pair_l)
    take(sent.at[9], cm_s.at[:, pl.ds(0, (n_tok - 1) * cols), :])
    partial = pl.ds(0, out_cols // 2)
    take(sent.at[10], one_a.at[:, pl.ds(1, lines - 1), :, :, partial])
    take(sent.at[11], one_b.at[:, pl.ds(1, n_head - 1), :, :, partial])
    take(sent.at[12], two_a.at[:, pl.ds(1, n_head - 1), :, partial])
    take(sent.at[13], two_b.at[:, pl.ds(1, lines - 1), :, partial])


def finish(out_v, ctx_v, com_v, out_ref, ctx_ref, com_ref, sems):
    copies = [
        pltpu.make_async_copy(src, dst, sems.at[i])
        for i, (src, dst) in enumerate(((out_v, out_ref), (com_v, com_ref), (ctx_v, ctx_ref)))
    ]
    for copy in copies:
        copy.start()
    for copy in copies:
        copy.wait()


def body(
    mamba_input, gate_input, in_b, in_c, step_size, decay_rate, skip_weight, norm_gain,
    ssm_state, out_weight, queries, draft_token_keys, draft_values, cached_key_rows,
    cache_values, cache_len, accepted,
):
    n_tok = lax.axis_size("tok")
    n_head = lax.axis_size("head")
    group = n_head * n_tok
    lines = n_tok // 2
    seqs, block, features = mamba_input.shape
    heads = decay_rate.shape[0]
    size = features // heads
    cols = ssm_state.shape[3]
    state = cols * n_tok
    draft = block * n_tok
    width = features // n_tok
    att = draft_token_keys.shape[2]
    per_kv = queries.shape[2] // att
    cache = cached_key_rows.shape[1]
    out_cols = out_weight.shape[1]
    per = draft // group
    chunks = 4
    hops = max(lines, n_head) - 1
    turned = jnp.transpose(ssm_state, (0, 1, 3, 2))
    shapes = (
        (per, seqs, out_cols),
        (seqs, block, per_kv * att),
        (seqs, heads, cols, size),
    )
    operands = (
        mamba_input, gate_input, in_b, in_c, step_size, turned, queries, cached_key_rows,
        cache_values, out_weight, draft_token_keys, draft_values,
        norm_gain.reshape(1, features), decay_rate, skip_weight, cache_len, accepted,
    )
    vmem = pl.BlockSpec(memory_space=pltpu.VMEM)
    held = pl.pallas_call(
        functools.partial(kernel, (n_head, n_tok, seqs, block, heads, chunks)),
        out_shape=[pltpu.VMEM(shape, BF16) for shape in shapes],
        in_specs=[pl.BlockSpec(memory_space=pltpu.HBM)] * len(operands),
        out_specs=[vmem] * 3,
        scratch_shapes=[
            pltpu.VMEM((seqs, 2, block, features), BF16),
            pltpu.VMEM((seqs, 2, draft, width), BF16),
            pltpu.VMEM((2, seqs, draft, state), BF16),
            pltpu.VMEM((seqs, draft, heads), BF16),
            pltpu.VMEM((seqs, heads, cols, size), BF16),
            pltpu.VMEM((seqs, cols, features), BF16),
            pltpu.VMEM((seqs, state, width), BF16),
            pltpu.VMEM((seqs, draft, per_kv * att), BF16),
            pltpu.VMEM((2, seqs, cache, att), BF16),
            pltpu.VMEM((2, seqs, block, att), BF16),
            pltpu.VMEM(out_weight.shape, BF16),
            pltpu.VMEM((1, features), F32),
            pltpu.VMEM((seqs, group, 1, draft), F32),
            pltpu.VMEM((seqs, state, width), BF16),
            pltpu.VMEM((seqs, cols, features), BF16),
            pltpu.VMEM((n_tok, seqs, per_kv * block, att), BF16),
            pltpu.VMEM((n_tok, seqs, per_kv * block, att), BF16),
            pltpu.VMEM((n_tok, seqs, per_kv * block), F32),
            pltpu.VMEM((n_tok, seqs, per_kv * block), F32),
            pltpu.VMEM((seqs, 2, n_head, lines, per, out_cols), BF16),
            pltpu.VMEM((seqs, n_head, lines, per, out_cols), BF16),
            pltpu.VMEM((seqs, n_head, lines, per, out_cols), BF16),
            pltpu.VMEM((seqs, lines, n_head, per, out_cols), BF16),
            pltpu.VMEM((seqs, n_head, lines, per, out_cols), BF16),
            pltpu.VMEM((seqs, n_head, per, out_cols), BF16),
            pltpu.VMEM((seqs, lines, per, out_cols), BF16),
            pltpu.VMEM((seqs, n_head, per, out_cols), BF16),
            pltpu.VMEM((seqs, lines, per, out_cols), BF16),
            pltpu.SMEM(decay_rate.shape, F32),
            pltpu.SMEM(skip_weight.shape, F32),
            pltpu.SMEM(cache_len.shape, jnp.int32),
            pltpu.SMEM(accepted.shape, jnp.int32),
            pltpu.SemaphoreType.DMA((14,)),
            pltpu.SemaphoreType.DMA((n_tok - 1,)),
            pltpu.SemaphoreType.DMA((lines,)),
            pltpu.SemaphoreType.DMA((lines,)),
            pltpu.SemaphoreType.DMA((seqs,)),
            pltpu.SemaphoreType.DMA((seqs,)),
            pltpu.SemaphoreType.DMA((3,)),
            pltpu.SemaphoreType.DMA((seqs,)),
            pltpu.SemaphoreType.DMA((seqs, chunks)),
            pltpu.SemaphoreType.DMA((seqs, chunks, hops)),
            pltpu.SemaphoreType.DMA((seqs, chunks, hops)),
            pltpu.SemaphoreType.DMA((13,)),
        ],
        compiler_params=pltpu.CompilerParams(
            collective_id=0, has_side_effects=True, vmem_limit_bytes=40 * 1024 * 1024
        ),
        name="hybrid",
    )(*[pltpu.with_memory_space_constraint(a, pltpu.HBM) for a in operands])
    out, ctx, com = pl.pallas_call(
        finish,
        out_shape=[jax.ShapeDtypeStruct(shape, BF16) for shape in shapes],
        in_specs=[vmem] * 3,
        out_specs=[pl.BlockSpec(memory_space=pl.ANY)] * 3,
        scratch_shapes=[pltpu.SemaphoreType.DMA((3,))],
        compiler_params=pltpu.CompilerParams(vmem_limit_bytes=4 * 1024 * 1024),
        name="finish",
    )(*[pltpu.with_memory_space_constraint(a, pltpu.VMEM) for a in held])
    return (out, ctx, jnp.transpose(com, (0, 1, 3, 2)))


def solution(mesh):
    in_specs = (
        P("dp", "tok", "head"),
        P("dp", "tok", "head"),
        P("dp", "tok", "head"),
        P("dp", "tok", "head"),
        P("dp", "tok", "head"),
        P("head"),
        P("head"),
        P("head"),
        P("dp", "head", None, "tok"),
        P(("head", "tok"), None),
        P("dp", "tok", "head"),
        P("dp", "tok", "head"),
        P("dp", "tok", "head"),
        P("dp", "tok", "head"),
        P("dp", "tok", "head"),
        P("dp"),
        P("dp"),
    )
    out_specs = (
        P(("head", "tok"), "dp", None),
        P("dp", "tok", "head"),
        P("dp", "head", None, "tok"),
    )
    return jax.shard_map(body, mesh=mesh, in_specs=in_specs, out_specs=out_specs, check_vma=False)
```

time: 23.4 us -> 22.4 us (0.957)
  Pallas kernels: 22.6 us -> 21.6 us
    pallas_call x1, Pallas kernels: 21.8 us -> 20.8 us  [body(): pl.pallas_call(functools.partial(kernel, (n_head, n_tok, seqs, block, hea...]
where the time goes in v2:
time: 22.4 us; the launch traced here: 22.3 us
  Pallas kernels  21.6 us (96%)
  between operations  0.65 us (3%)
    pallas_call x1, Pallas kernels, body(): pl.pallas_call(functools.partial(kernel, (n_head, n_tok, seqs, block, hea...  20.8 us
    pallas_call x1, Pallas kernels, body(): pl.pallas_call(finish, out_shape=[jax.ShapeDtypeStruct(shape, BF16) for s...  0.78 us

profile of v2, /device:TPU:0, one launch (start us, length us, event | category | flops | bytes accessed | tf_op | source)
XLA Modules:
  0.0 22.3 jit_solution(14665121692629646262)
XLA Ops:
  0.6 20.8 %hybrid.1 = (bf16[8,2,4096]{2,1,0:T(2,128)(2,1)S(1)}, bf16[2,16,512]{2,1,0:T(8,128)(2,1)S(1)}, bf16[2,16,32,64]{3,2,1,0:T(8,128)(2,1)S(1)}) custom-call(bf16[2,16,1024]{2,1,0:T(8,128)(2,1)} %x_in.1, bf16[2,16,1024]{2,1,0:T(8,128)(2,1)} %z_in.1, bf16[2,16,128]{2,1,0:T(8,128)(2,1)} %b_in.1, bf16[2,16,128]{2,1,0:T(8,128)(2,1)} %c_in.1, ...), custom_call_target="tpu_custom_call" | custom-call | tf_op jit(solution)/shard_map/hybrid/pallas_call | solution.py:485
  21.5 0.8 %finish.1 = (bf16[8,2,4096]{2,1,0:T(2,128)(2,1)}, bf16[2,16,512]{2,1,0:T(8,128)(2,1)}, bf16[2,16,32,64]{3,2,1,0:T(8,128)(2,1)}) custom-call(bf16[8,2,4096]{2,1,0:T(2,128)(2,1)S(1)} %get-tuple-element.9.out_v, bf16[2,16,512]{2,1,0:T(8,128)(2,1)S(1)} %get-tuple-element.10.ctx_v, bf16[2,16,32,64]{3,2,1,0:T(8,128)(2,1)S(1)} %get-tuple-element.11.com_v), custom_call_target="tpu_custom_call" | custom-call | tf_op jit(solution)/shard_map/finish/pallas_call | solution.py:541

commit v3 on v2

--- a/solution.py
+++ b/solution.py
@@ -128,8 +128,14 @@
             if only is None or kind in only:
                 remote(kind, ref, ref, recv, device)
 
+    def across(o):
+        return lax.rem(line + o, lines) * 2 + lax.rem(side + o, 2)
+
+    def origin(o, near):
+        return lax.rem(line - o + lines, lines) * 2 + lax.rem(near + o, 2)
+
     for o in range(1, lines):
-        share(tok, {"tok": lax.rem(line + o, lines) * 2 + side}, o, o)
+        share(tok, {"tok": across(o)}, o, o)
     share(tok, partner, 0, 0)
     for s in range(seqs):
         for o in range(1, n_tok):
@@ -150,21 +156,23 @@
     take(local.at[5], new_v)
     take(local.at[6], kv_v)
     scale = att ** (-0.5)
+    pair = 2 * block
     m_own = per_kv * block
-    eye = iota((m_own, m_own), 0) == iota((m_own, m_own), 1)
+    m_pair = per_kv * pair
+    eye = iota((m_pair, m_pair), 0) == iota((m_pair, m_pair), 1)
     position = tok * cache + iota((1, cache), 1)
-    inner = iota((block, block), 1) - iota((block, block), 0)
+    inner = iota((pair, block), 1) - iota((pair, block), 0)
     inner = jnp.concatenate([inner] * per_kv, axis=0)
 
-    def attend(t, n_to, stat_to):
+    def attend(at):
         for s in range(seqs):
             q = jnp.concatenate(
-                [q_l[s, place(t, block), h * att : (h + 1) * att] for h in range(per_kv)], axis=0
+                [q_l[s, place(at, pair), h * att : (h + 1) * att] for h in range(per_kv)], axis=0
             )
             old = lax.dot_general(q, kv_v[0, s], NT, preferred_element_type=F32)
             old = jnp.where(position < len_ref[s], old, MASKED)
             new = lax.dot_general(q, new_v[0, s], NT, preferred_element_type=F32)
-            new = jnp.where(inner <= (t - tok) * block, new, MASKED)
+            new = jnp.where(inner <= at * pair - tok * block, new, MASKED)
             peak = jnp.maximum(
                 jnp.max(old, axis=1, keepdims=True), jnp.max(new, axis=1, keepdims=True)
             )
@@ -175,31 +183,35 @@
             numer = dot(old.astype(BF16), kv_v[1, s]) + dot(new.astype(BF16), new_v[1, s])
             safe = jnp.maximum(total, 1e-30)
             level = jnp.where(total > 0.0, peak * scale + jnp.log(safe), MASKED)
-            n_to[s] = (numer / safe).astype(BF16)
-            stat_to[s : s + 1, :] = jnp.sum(jnp.where(eye, level, 0.0), axis=0, keepdims=True)
-
-    def attend_for(t, index):
-        attend(t, n_s.at[index], stat_s.at[index])
-        remote(5, n_s.at[index], n_l.at[tok], got.at[0], {"tok": t})
-        remote(6, stat_s.at[index], stat_l.at[tok], got.at[1], {"tok": t})
-
-    attend(tok, n_l.at[tok], stat_l.at[tok])
+            ctx = (numer / safe).astype(BF16)
+            for c in range(2):
+                for h in range(per_kv):
+                    n_s[at * 2 + c, s, h * block : (h + 1) * block] = ctx[
+                        (h * 2 + c) * block : (h * 2 + c + 1) * block
+                    ]
+            stat_s[at, s : s + 1, :] = jnp.sum(jnp.where(eye, level, 0.0), axis=0, keepdims=True)
+
+    def answer(t):
+        remote(5, n_s.at[t], n_l.at[tok], got.at[0], {"tok": t})
+        remote(6, stat_s.at[t // 2], stat_l.at[tok], got.at[1], {"tok": t})
+
     take(q_recv.at[0], q_l.at[:, mine, :])
-    attend_for(flip, 0)
+    attend(line)
+    answer(flip)
+    n_l[tok] = n_s[tok]
+    stat_l[tok] = stat_s[line]
     for o in range(1, lines):
-        origin = lax.rem(line - o + lines, lines) * 2 + side
         take(q_recv.at[o], q_l.at[:, mine, :])
-        share(origin, partner, lines - 1 + o, 0, (0,))
+        share(origin(o, side), partner, lines - 1 + o, 0, (0,))
     for o in range(1, lines):
-        origin = lax.rem(line - o + lines, lines) * 2 + side
         take(bc_recv.at[o], bc_l.at[:, :, mine, :])
         take(dt_recv.at[o], dt_l.at[:, mine, :])
-        share(origin, partner, 0, 0, (1, 2))
-    for o in range(1, lines):
-        attend_for(lax.rem(line - o + lines, lines) * 2 + side, o)
+        share(origin(o, side), partner, 0, 0, (1, 2))
     for o in range(1, lines):
         take(q_recv.at[lines - 1 + o], q_l.at[:, mine, :])
-        attend_for(lax.rem(line - o + lines, lines) * 2 + 1 - side, lines - 1 + o)
+        attend(lax.rem(line - o + lines, lines))
+        answer(origin(o, side))
+        answer(origin(o, 1 - side))
 
     lane = iota((1, width), 1)
     rate_x = jnp.zeros((1, width), F32)
@@ -213,22 +225,23 @@
     causal = iota((draft, draft), 0) >= iota((draft, draft), 1)
     lower = causal.astype(F32).astype(BF16)
 
-    def target(dim):
-        source = iota((draft, draft), dim)
-        result = jnp.zeros((draft, draft), jnp.int32)
-        for g in range(group):
-            base = (g % 2) * (draft // 2) + (g // 2) * per
-            inside = (source >= g * per) & (source < (g + 1) * per)
-            result = jnp.where(inside, source - g * per + base, result)
-        return result
-
-    swap = (iota((draft, draft), 0) == target(1)).astype(F32).astype(BF16)
-    moved = target(0) == iota((draft, draft), 1)
+    level_eye = iota((draft, draft), 0) == iota((draft, draft), 1)
     take(local.at[11], gain_v)
     gain = gain_v[:, place(tok, width)]
     take(local.at[12], w_v)
     take(bc_recv.at[0], bc_l.at[:, :, pl.ds(0, lines * block), :])
     take(dt_recv.at[0], dt_l.at[:, pl.ds(0, lines * block), :])
+    early = []
+    for s in range(seqs):
+        dtx = dot(dt_l[s], pick)
+        run = -rate_x * dot(lower, dtx.astype(BF16))
+        mix = lax.dot_general(bc_l[1, s], bc_l[0, s], NT, preferred_element_type=F32)
+        mix = jnp.where(causal, mix, 0.0).astype(BF16)
+        alive = iota((draft, width), 0) < acc_ref[s]
+        end = -rate_x * jnp.sum(jnp.where(alive, dtx, 0.0), axis=0, keepdims=True)
+        weight = jnp.where(alive, jnp.exp(jnp.where(alive, end - run, 0.0)) * dtx, 0.0)
+        flow = bc_l[0, s].astype(F32).T.astype(BF16)
+        early.append((mix, jnp.exp(run), dtx * jnp.exp(-run), weight, jnp.exp(end), flow))
 
     tile = min(512, span)
 
@@ -238,31 +251,31 @@
     def mix_tokens(s):
         x = xz_l[s, 0].astype(F32)
         z = xz_l[s, 1].astype(F32)
-        dtx = dot(dt_l[s], pick)
-        run = -rate_x * dot(lower, dtx.astype(BF16))
-        scaled = (x * dtx * jnp.exp(-run)).astype(BF16)
-        mix = lax.dot_general(bc_l[1, s], bc_l[0, s], NT, preferred_element_type=F32)
-        mix = jnp.where(causal, mix, 0.0).astype(BF16)
-        y = jnp.exp(run) * (dot(mix, scaled) + dot(bc_l[1, s], st_l[s])) + skip_x * x
+        mix, grown, shrunk = early[s][:3]
+        inside = dot(mix, (x * shrunk).astype(BF16))
+        y = grown * (inside + dot(bc_l[1, s], st_l[s])) + skip_x * x
         gated = y * z / (1.0 + jnp.exp(-z))
+        return x, gated
+
+    def spread(s, gated):
         sums = jnp.sum(gated * gated, axis=1, keepdims=True)
-        ss_l[s, me] = jnp.sum(jnp.where(moved, sums, 0.0), axis=0, keepdims=True)
+        ss_l[s, me] = jnp.sum(jnp.where(level_eye, sums, 0.0), axis=0, keepdims=True)
         for o in range(1, group):
             peer = lax.rem(me + o, group)
             remote(
                 7, ss_l.at[s, me], ss_l.at[s, me], ss_recv.at[s],
                 {"head": peer // n_tok, "tok": lax.rem(peer, n_tok)},
             )
-        return dot(swap, (gated * gain).astype(BF16)).astype(BF16), (x, dtx, run)
 
     def project(s, normed):
         for ch in range(chunks):
             for start in range(ch * span, (ch + 1) * span, tile):
                 val = dot(normed, w_v[:, start : start + tile])
-                for p in range(2):
-                    for g in range(half):
-                        at = (p * half + g) * per
-                        part[s, p, g // lines, g % lines, :, start : start + tile] = val[
+                for g in range(half):
+                    for p in range(2):
+                        at = (g * 2 + p) * per
+                        hold = lax.rem(p + head + line + g // lines + g % lines, 2)
+                        part[s, hold, g // lines, g % lines, :, start : start + tile] = val[
                             at : at + per
                         ].astype(BF16)
             remote(
@@ -270,13 +283,9 @@
                 pair_l.at[s, :, :, :, piece_of(ch)], pair_recv.at[s, ch], partner,
             )
 
-    def commit(s, saved):
-        x, dtx, run = saved
-        alive = iota((draft, width), 0) < acc_ref[s]
-        end = -rate_x * jnp.sum(jnp.where(alive, dtx, 0.0), axis=0, keepdims=True)
-        weight = jnp.where(alive, jnp.exp(jnp.where(alive, end - run, 0.0)) * dtx, 0.0)
-        flow = bc_l[0, s].astype(F32).T.astype(BF16)
-        new = jnp.exp(end) * st_l[s].astype(F32) + dot(flow, (x * weight).astype(BF16))
+    def commit(s, x):
+        weight, decay, flow = early[s][3:]
+        new = decay * st_l[s].astype(F32) + dot(flow, (x * weight).astype(BF16))
         cm_s[s] = new.astype(BF16)
         for o in range(1, n_tok):
             to = lax.rem(tok + o, n_tok)
@@ -285,6 +294,9 @@
                 got.at[2], {"tok": to},
             )
         cm_l[s, :, place(tok, width)] = cm_s[s, place(tok, cols), :]
+
+    def above(o):
+        return {"head": lax.rem(head + o, n_head), "tok": line * 2 + lax.rem(side + o, 2)}
 
     def line_first(ch):
         return ch % 2 == 0
@@ -300,21 +312,21 @@
                 to = lax.rem(line + o, lines)
                 remote(
                     10, red.at[s, :, to, :, piece], one_a.at[s, o, :, :, piece],
-                    one_recv.at[s, ch, o - 1], {"tok": to * 2 + side},
+                    one_recv.at[s, ch, o - 1], {"tok": across(o)},
                 )
         else:
             for o in range(1, n_head):
                 to = lax.rem(head + o, n_head)
                 remote(
                     11, red.at[s, to, :, :, piece], one_b.at[s, o, :, :, piece],
-                    one_recv.at[s, ch, o - 1], {"head": to},
+                    one_recv.at[s, ch, o - 1], above(o),
                 )
 
-    def factor(s, origin, base, count):
+    def factor(s, source, base):
         total = jnp.zeros((1, draft), F32)
         for t in range(n_tok):
-            total = total + ss_l[s, origin * n_tok + t]
-        here = iota((count, draft), 1) == base + iota((count, draft), 0)
+            total = total + ss_l[s, source * n_tok + t]
+        here = iota((per, draft), 1) == base * per + iota((per, draft), 0)
         column = jnp.sum(jnp.where(here, total, 0.0), axis=1, keepdims=True)
         return lax.rsqrt(column / (width * n_tok) + EPSILON)
 
@@ -331,22 +343,21 @@
                 to = lax.rem(head + o, n_head)
                 remote(
                     12, mid_a.at[s, to, :, piece], two_a.at[s, o, :, piece],
-                    two_recv.at[s, ch, o - 1], {"head": to},
+                    two_recv.at[s, ch, o - 1], above(o),
                 )
         else:
             for o in range(1, n_head):
                 take(one_recv.at[s, ch, o - 1], one_b.at[s, o, :, :, piece])
             for l in range(lines):
-                near = slice(l * per, (l + 1) * per)
-                total = red[s, head, l, :, piece].astype(F32) * factors[0][near]
+                total = red[s, head, l, :, piece].astype(F32) * factors[0][l]
                 for o in range(1, n_head):
-                    total = total + one_b[s, o, l, :, piece].astype(F32) * factors[o][near]
+                    total = total + one_b[s, o, l, :, piece].astype(F32) * factors[o][l]
                 mid_b[s, l, :, piece] = total.astype(BF16)
             for o in range(1, lines):
                 to = lax.rem(line + o, lines)
                 remote(
                     13, mid_b.at[s, to, :, piece], two_b.at[s, o, :, piece],
-                    two_recv.at[s, ch, o - 1], {"tok": to * 2 + side},
+                    two_recv.at[s, ch, o - 1], {"tok": across(o)},
                 )
 
     def final(s, ch, factors):
@@ -368,17 +379,25 @@
     for s in range(seqs):
         take(st_recv.at[s], st_l.at[s, pl.ds(0, (n_tok - 1) * cols), :])
         take(xz_recv.at[s], xz_l.at[s, :, pl.ds(0, (n_tok - 1) * block), :])
-        normed, saved = mix_tokens(s)
-        project(s, normed)
-        commit(s, saved)
+        x, gated = mix_tokens(s)
+        project(s, (gated * gain).astype(BF16))
+        spread(s, gated)
+        commit(s, x)
         for ch in range(chunks):
             forward(s, ch)
 
     take(got.at[0], n_l.at[pl.ds(0, n_tok - 1)])
     take(got.at[1], stat_l.at[pl.ds(0, n_tok - 1)])
+    lanes = iota((m_own, m_pair), 1)
+    r = iota((m_own, m_pair), 0)
+    want = None
+    for h in range(per_kv):
+        t = r - h * block
+        hit = (t >= 0) & (t < block) & (lanes == h * pair + side * block + t)
+        want = hit if want is None else want | hit
     for s in range(seqs):
         levels = [
-            jnp.sum(jnp.where(eye, stat_l[t, s : s + 1, :], 0.0), axis=1, keepdims=True)
+            jnp.sum(jnp.where(want, stat_l[t, s : s + 1, :], 0.0), axis=1, keepdims=True)
             for t in range(n_tok)
         ]
         top = functools.reduce(jnp.maximum, levels)
@@ -391,13 +410,13 @@
         for h in range(per_kv):
             ctx_ref[s, :, h * att : (h + 1) * att] = acc[h * block : (h + 1) * block]
 
-    ours = side * (draft // 2) + head * lines * per
     narrow = []
     for s in range(seqs):
         take(ss_recv.at[s], ss_l.at[s, pl.ds(0, group - 1)])
-        origins = [lax.rem(head - o + n_head, n_head) for o in range(n_head)]
-        wide = [factor(s, origin, ours, lines * per) for origin in origins]
-        narrow.append([factor(s, origin, ours + line * per, per) for origin in origins])
+        sources = [lax.rem(head - o + n_head, n_head) for o in range(n_head)]
+        places = [(head * lines + l) * 2 + lax.rem(side + line + l, 2) for l in range(lines)]
+        wide = [[factor(s, source, at) for at in places] for source in sources]
+        narrow.append([factor(s, source, me) for source in sources])
         for ch in range(chunks):
             second(s, ch, wide)
 
@@ -425,7 +444,7 @@
     take(sent.at[3], turn_v.at[:, :, pl.ds(0, (n_tok - 1) * width)])
     take(sent.at[4], xz_v.at[:, :, :, pl.ds(0, (n_tok - 1) * width)])
     take(sent.at[5], n_s.at[others])
-    take(sent.at[6], stat_s.at[others])
+    take(sent.at[6], stat_l.at[others])
     take(sent.at[7], ss_l.at[:, pl.ds(0, group - 1)])
     take(sent.at[8], pair_l)
     take(sent.at[9], cm_s.at[:, pl.ds(0, (n_tok - 1) * cols), :])
@@ -505,8 +524,8 @@
             pltpu.VMEM((seqs, cols, features), BF16),
             pltpu.VMEM((n_tok, seqs, per_kv * block, att), BF16),
             pltpu.VMEM((n_tok, seqs, per_kv * block, att), BF16),
-            pltpu.VMEM((n_tok, seqs, per_kv * block), F32),
-            pltpu.VMEM((n_tok, seqs, per_kv * block), F32),
+            pltpu.VMEM((lines, seqs, 2 * per_kv * block), F32),
+            pltpu.VMEM((n_tok, seqs, 2 * per_kv * block), F32),
             pltpu.VMEM((seqs, 2, n_head, lines, per, out_cols), BF16),
             pltpu.VMEM((seqs, n_head, lines, per, out_cols), BF16),
             pltpu.VMEM((seqs, n_head, lines, per, out_cols), BF16),

time: 22.4 us -> 21 us (0.938)
  Pallas kernels: 21.6 us -> 20.2 us
    pallas_call x1, Pallas kernels: 20.8 us -> 19.4 us  [body(): pl.pallas_call(functools.partial(kernel, (n_head, n_tok, seqs, block, hea...]
where the time goes in v3:
time: 21 us; the launch traced here: 20.9 us
  Pallas kernels  20.2 us (96%)
  between operations  0.65 us (3%)
    pallas_call x1, Pallas kernels, body(): pl.pallas_call(functools.partial(kernel, (n_head, n_tok, seqs, block, hea...  19.4 us
    pallas_call x1, Pallas kernels, body(): pl.pallas_call(finish, out_shape=[jax.ShapeDtypeStruct(shape, BF16) for s...  0.78 us

profile of v3, /device:TPU:0, one launch (start us, length us, event | category | flops | bytes accessed | tf_op | source)
XLA Modules:
  0.0 20.9 jit_solution(18430394604267458553)
XLA Ops:
  0.6 19.4 %hybrid.1 = (bf16[8,2,4096]{2,1,0:T(2,128)(2,1)S(1)}, bf16[2,16,512]{2,1,0:T(8,128)(2,1)S(1)}, bf16[2,16,32,64]{3,2,1,0:T(8,128)(2,1)S(1)}) custom-call(bf16[2,16,1024]{2,1,0:T(8,128)(2,1)} %x_in.1, bf16[2,16,1024]{2,1,0:T(8,128)(2,1)} %z_in.1, bf16[2,16,128]{2,1,0:T(8,128)(2,1)} %b_in.1, bf16[2,16,128]{2,1,0:T(8,128)(2,1)} %c_in.1, ...), custom_call_target="tpu_custom_call" | custom-call | tf_op jit(solution)/shard_map/hybrid/pallas_call | solution.py:504
  20.1 0.8 %finish.1 = (bf16[8,2,4096]{2,1,0:T(2,128)(2,1)}, bf16[2,16,512]{2,1,0:T(8,128)(2,1)}, bf16[2,16,32,64]{3,2,1,0:T(8,128)(2,1)}) custom-call(bf16[8,2,4096]{2,1,0:T(2,128)(2,1)S(1)} %get-tuple-element.9.out_v, bf16[2,16,512]{2,1,0:T(8,128)(2,1)S(1)} %get-tuple-element.10.ctx_v, bf16[2,16,32,64]{3,2,1,0:T(8,128)(2,1)S(1)} %get-tuple-element.11.com_v), custom_call_target="tpu_custom_call" | custom-call | tf_op jit(solution)/shard_map/finish/pallas_call | solution.py:560

commit v4 on v3

--- a/solution.py
+++ b/solution.py
@@ -23,19 +23,28 @@
     return lax.broadcasted_iota(jnp.int32, shape, dim)
 
 
+PLAN = ("ABAB", "ABAB")
+EARLY = (0,)
+LATE = 0
+WEAVE = 2
+
+
 def kernel(
     dims,
     x_in, z_in, b_in, c_in, dt_in, st_in, q_in, k_in, v_in, w_in,
     dk_in, dv_in, gain_in, rate_in, skip_in, len_in, acc_in,
     out_ref, ctx_ref, com_ref,
-    xz_v, xz_l, bc_l, dt_l, raw_v, turn_v, st_l, q_l, kv_v, new_v, w_v, gain_v,
+    xz_v, xz_l, bc_l, dt_v, raw_v, turn_v, st_l, q_l, kv_v, new_v, w_v, gain_v,
     ss_l, cm_s, cm_l, n_s, n_l, stat_s, stat_l,
     part, pair_l, red, one_a, one_b, mid_a, mid_b, two_a, two_b,
-    rate_ref, skip_ref, len_ref, acc_ref,
-    sent, q_recv, bc_recv, dt_recv, st_recv, xz_recv, got, ss_recv,
+    heads_ref, seqs_ref,
+    sent, q_recv, bc_recv, st_recv, xz_recv, got, ss_recv,
     pair_recv, one_recv, two_recv, local,
 ):
-    n_head, n_tok, seqs, block, heads, chunks = dims
+    n_head, n_tok, seqs, block, heads, plan = dims
+    chunks = len(plan[0])
+    counts = [row.count("A") for row in plan]
+    kinds = [sorted(set(counts)).index(count) for count in counts]
     group = n_head * n_tok
     tok = lax.axis_index("tok")
     head = lax.axis_index("head")
@@ -79,19 +88,19 @@
         (1, q_in, q_l.at[:, mine, :]),
         (2, b_in, bc_l.at[0, :, mine, :]),
         (2, c_in, bc_l.at[1, :, mine, :]),
-        (3, dt_in, dt_l.at[:, mine, :]),
+        (3, dt_in, dt_v),
         (4, x_in, xz_v.at[:, 0]),
         (4, z_in, xz_v.at[:, 1]),
         (5, dk_in, new_v.at[0]),
         (5, dv_in, new_v.at[1]),
         (6, k_in, kv_v.at[0]),
         (6, v_in, kv_v.at[1]),
-        (7, len_in, len_ref),
-        (8, acc_in, acc_ref),
-        (9, rate_in, rate_ref),
-        (10, skip_in, skip_ref),
-        (11, gain_in, gain_v),
-        (12, w_in, w_v),
+        (7, len_in, seqs_ref.at[0]),
+        (7, acc_in, seqs_ref.at[1]),
+        (8, rate_in, heads_ref.at[0]),
+        (8, skip_in, heads_ref.at[1]),
+        (9, gain_in, gain_v),
+        (10, w_in, w_v),
     ):
         pltpu.make_async_copy(src, dst, local.at[sem]).start()
 
@@ -102,8 +111,10 @@
         ).astype(BF16)
     st_l[:, place(tok, cols), :] = turn_v[:, :, place(tok, width)]
     take(local.at[1], q_l.at[:, mine, :])
-    take(local.at[2], bc_l.at[:, :, mine, :])
-    take(local.at[3], dt_l.at[:, mine, :])
+    take(local.at[2], bc_l.at[pl.ds(0, 2), :, mine, :])
+    take(local.at[3], dt_v)
+    pad = jnp.zeros((seqs, block, state - heads), BF16)
+    bc_l[2, :, mine, :] = jnp.concatenate([dt_v[...], pad], axis=2)
     take(local.at[4], xz_v)
     xz_l[:, :, mine, :] = xz_v[:, :, :, place(tok, width)]
 
@@ -123,7 +134,6 @@
         for kind, ref, recv in (
             (0, q_l.at[:, span_at, :], q_recv.at[q_sem]),
             (1, bc_l.at[:, :, span_at, :], bc_recv.at[sem]),
-            (2, dt_l.at[:, span_at, :], dt_recv.at[sem]),
         ):
             if only is None or kind in only:
                 remote(kind, ref, ref, recv, device)
@@ -151,28 +161,36 @@
                 xz_recv.at[s], {"tok": to},
             )
 
-    for i, ref in ((7, len_ref), (8, acc_ref), (9, rate_ref), (10, skip_ref)):
-        take(local.at[i], ref)
+    take(local.at[7], seqs_ref)
+    take(local.at[8], heads_ref)
     take(local.at[5], new_v)
     take(local.at[6], kv_v)
     scale = att ** (-0.5)
-    pair = 2 * block
     m_own = per_kv * block
-    m_pair = per_kv * pair
-    eye = iota((m_pair, m_pair), 0) == iota((m_pair, m_pair), 1)
+    eye = iota((m_own, m_own), 0) == iota((m_own, m_own), 1)
     position = tok * cache + iota((1, cache), 1)
-    inner = iota((pair, block), 1) - iota((pair, block), 0)
-    inner = jnp.concatenate([inner] * per_kv, axis=0)
-
-    def attend(at):
+
+    def attend(at, count):
+        first, height = at * count, count * block
+        inner = iota((height, block), 1) - iota((height, block), 0)
+        inner = jnp.concatenate([inner] * per_kv, axis=0)
+        r, lanes = (iota((per_kv * height, m_own), d) for d in range(2))
+        picks = []
+        for c in range(count):
+            pick = None
+            for h in range(per_kv):
+                t = r - (h * count + c) * block
+                hit = (t >= 0) & (t < block) & (lanes == h * block + t)
+                pick = hit if pick is None else pick | hit
+            picks.append(pick)
         for s in range(seqs):
             q = jnp.concatenate(
-                [q_l[s, place(at, pair), h * att : (h + 1) * att] for h in range(per_kv)], axis=0
+                [q_l[s, place(at, height), h * att : (h + 1) * att] for h in range(per_kv)], axis=0
             )
             old = lax.dot_general(q, kv_v[0, s], NT, preferred_element_type=F32)
-            old = jnp.where(position < len_ref[s], old, MASKED)
+            old = jnp.where(position < seqs_ref[0, s], old, MASKED)
             new = lax.dot_general(q, new_v[0, s], NT, preferred_element_type=F32)
-            new = jnp.where(inner <= at * pair - tok * block, new, MASKED)
+            new = jnp.where(inner <= (first - tok) * block, new, MASKED)
             peak = jnp.maximum(
                 jnp.max(old, axis=1, keepdims=True), jnp.max(new, axis=1, keepdims=True)
             )
@@ -184,33 +202,36 @@
             safe = jnp.maximum(total, 1e-30)
             level = jnp.where(total > 0.0, peak * scale + jnp.log(safe), MASKED)
             ctx = (numer / safe).astype(BF16)
-            for c in range(2):
+            for c in range(count):
                 for h in range(per_kv):
-                    n_s[at * 2 + c, s, h * block : (h + 1) * block] = ctx[
-                        (h * 2 + c) * block : (h * 2 + c + 1) * block
+                    n_s[first + c, s, h * block : (h + 1) * block] = ctx[
+                        (h * count + c) * block : (h * count + c + 1) * block
                     ]
-            stat_s[at, s : s + 1, :] = jnp.sum(jnp.where(eye, level, 0.0), axis=0, keepdims=True)
+                stat_s[first + c, s] = jnp.sum(
+                    jnp.where(picks[c], level, 0.0), axis=0, keepdims=True
+                )
 
     def answer(t):
         remote(5, n_s.at[t], n_l.at[tok], got.at[0], {"tok": t})
-        remote(6, stat_s.at[t // 2], stat_l.at[tok], got.at[1], {"tok": t})
+        remote(6, stat_s.at[t], stat_l.at[tok], got.at[1], {"tok": t})
 
     take(q_recv.at[0], q_l.at[:, mine, :])
-    attend(line)
+    attend(line, 2)
     answer(flip)
     n_l[tok] = n_s[tok]
-    stat_l[tok] = stat_s[line]
+    stat_l[tok] = stat_s[tok]
     for o in range(1, lines):
         take(q_recv.at[o], q_l.at[:, mine, :])
         share(origin(o, side), partner, lines - 1 + o, 0, (0,))
     for o in range(1, lines):
+        attend(origin(o, side), 1)
+        answer(origin(o, side))
+    for o in range(1, lines):
         take(bc_recv.at[o], bc_l.at[:, :, mine, :])
-        take(dt_recv.at[o], dt_l.at[:, mine, :])
-        share(origin(o, side), partner, 0, 0, (1, 2))
+        share(origin(o, side), partner, 0, 0, (1,))
     for o in range(1, lines):
         take(q_recv.at[lines - 1 + o], q_l.at[:, mine, :])
-        attend(lax.rem(line - o + lines, lines))
-        answer(origin(o, side))
+        attend(origin(o, 1 - side), 1)
         answer(origin(o, 1 - side))
 
     lane = iota((1, width), 1)
@@ -218,30 +239,32 @@
     skip_x = jnp.zeros((1, width), F32)
     for h in range(own):
         inside = (lane >= h * size) & (lane < (h + 1) * size)
-        rate_x = jnp.where(inside, rate_ref[tok * own + h], rate_x)
-        skip_x = jnp.where(inside, skip_ref[tok * own + h], skip_x)
-    offset = iota((heads, width), 1) - (iota((heads, width), 0) - tok * own) * size
+        rate_x = jnp.where(inside, heads_ref[0, tok * own + h], rate_x)
+        skip_x = jnp.where(inside, heads_ref[1, tok * own + h], skip_x)
+    offset = iota((state, width), 1) - (iota((state, width), 0) - tok * own) * size
     pick = ((offset >= 0) & (offset < size)).astype(F32).astype(BF16)
     causal = iota((draft, draft), 0) >= iota((draft, draft), 1)
     lower = causal.astype(F32).astype(BF16)
 
     level_eye = iota((draft, draft), 0) == iota((draft, draft), 1)
-    take(local.at[11], gain_v)
+    take(local.at[9], gain_v)
     gain = gain_v[:, place(tok, width)]
-    take(local.at[12], w_v)
+    take(local.at[10], w_v)
     take(bc_recv.at[0], bc_l.at[:, :, pl.ds(0, lines * block), :])
-    take(dt_recv.at[0], dt_l.at[:, pl.ds(0, lines * block), :])
-    early = []
-    for s in range(seqs):
-        dtx = dot(dt_l[s], pick)
+    early = {}
+
+    def prepare(s):
+        dtx = dot(bc_l[2, s], pick)
         run = -rate_x * dot(lower, dtx.astype(BF16))
         mix = lax.dot_general(bc_l[1, s], bc_l[0, s], NT, preferred_element_type=F32)
         mix = jnp.where(causal, mix, 0.0).astype(BF16)
-        alive = iota((draft, width), 0) < acc_ref[s]
+        alive = iota((draft, width), 0) < seqs_ref[1, s]
         end = -rate_x * jnp.sum(jnp.where(alive, dtx, 0.0), axis=0, keepdims=True)
         weight = jnp.where(alive, jnp.exp(jnp.where(alive, end - run, 0.0)) * dtx, 0.0)
         flow = bc_l[0, s].astype(F32).T.astype(BF16)
-        early.append((mix, jnp.exp(run), dtx * jnp.exp(-run), weight, jnp.exp(end), flow))
+        early[s] = (mix, jnp.exp(run), dtx * jnp.exp(-run), weight, jnp.exp(end), flow)
+
+    prepare(0)
 
     tile = min(512, span)
 
@@ -267,7 +290,7 @@
                 {"head": peer // n_tok, "tok": lax.rem(peer, n_tok)},
             )
 
-    def project(s, normed):
+    def project(s, normed, between):
         for ch in range(chunks):
             for start in range(ch * span, (ch + 1) * span, tile):
                 val = dot(normed, w_v[:, start : start + tile])
@@ -282,24 +305,24 @@
                 8, part.at[s, 1 - side, :, :, :, piece_of(ch)],
                 pair_l.at[s, :, :, :, piece_of(ch)], pair_recv.at[s, ch], partner,
             )
+            between(ch)
 
     def commit(s, x):
         weight, decay, flow = early[s][3:]
         new = decay * st_l[s].astype(F32) + dot(flow, (x * weight).astype(BF16))
         cm_s[s] = new.astype(BF16)
+        cm_l[s, :, place(tok, width)] = cm_s[s, place(tok, cols), :]
+
+    def hand_out(s):
         for o in range(1, n_tok):
             to = lax.rem(tok + o, n_tok)
             remote(
                 9, cm_s.at[s, place(to, cols), :], cm_l.at[s, :, place(tok, width)],
                 got.at[2], {"tok": to},
             )
-        cm_l[s, :, place(tok, width)] = cm_s[s, place(tok, cols), :]
 
     def above(o):
         return {"head": lax.rem(head + o, n_head), "tok": line * 2 + lax.rem(side + o, 2)}
-
-    def line_first(ch):
-        return ch % 2 == 0
 
     def forward(s, ch):
         piece = piece_of(ch)
@@ -307,18 +330,18 @@
         red[s, :, :, :, piece] = (
             part[s, side, :, :, :, piece].astype(F32) + pair_l[s, :, :, :, piece].astype(F32)
         ).astype(BF16)
-        if line_first(ch):
+        if plan[s][ch] == "A":
             for o in range(1, lines):
                 to = lax.rem(line + o, lines)
                 remote(
-                    10, red.at[s, :, to, :, piece], one_a.at[s, o, :, :, piece],
+                    10 + 4 * kinds[s], red.at[s, :, to, :, piece], one_a.at[s, o, :, :, piece],
                     one_recv.at[s, ch, o - 1], {"tok": across(o)},
                 )
         else:
             for o in range(1, n_head):
                 to = lax.rem(head + o, n_head)
                 remote(
-                    11, red.at[s, to, :, :, piece], one_b.at[s, o, :, :, piece],
+                    11 + 4 * kinds[s], red.at[s, to, :, :, piece], one_b.at[s, o, :, :, piece],
                     one_recv.at[s, ch, o - 1], above(o),
                 )
 
@@ -332,7 +355,7 @@
 
     def second(s, ch, factors):
         piece = piece_of(ch)
-        if line_first(ch):
+        if plan[s][ch] == "A":
             for o in range(1, lines):
                 take(one_recv.at[s, ch, o - 1], one_a.at[s, o, :, :, piece])
             total = red[s, :, line, :, piece].astype(F32)
@@ -342,7 +365,7 @@
             for o in range(1, n_head):
                 to = lax.rem(head + o, n_head)
                 remote(
-                    12, mid_a.at[s, to, :, piece], two_a.at[s, o, :, piece],
+                    12 + 4 * kinds[s], mid_a.at[s, to, :, piece], two_a.at[s, o, :, piece],
                     two_recv.at[s, ch, o - 1], above(o),
                 )
         else:
@@ -356,13 +379,13 @@
             for o in range(1, lines):
                 to = lax.rem(line + o, lines)
                 remote(
-                    13, mid_b.at[s, to, :, piece], two_b.at[s, o, :, piece],
+                    13 + 4 * kinds[s], mid_b.at[s, to, :, piece], two_b.at[s, o, :, piece],
                     two_recv.at[s, ch, o - 1], {"tok": across(o)},
                 )
 
     def final(s, ch, factors):
         piece = piece_of(ch)
-        if line_first(ch):
+        if plan[s][ch] == "A":
             for o in range(1, n_head):
                 take(two_recv.at[s, ch, o - 1], two_a.at[s, o, :, piece])
             total = mid_a[s, head, :, piece].astype(F32) * factors[0]
@@ -380,24 +403,44 @@
         take(st_recv.at[s], st_l.at[s, pl.ds(0, (n_tok - 1) * cols), :])
         take(xz_recv.at[s], xz_l.at[s, :, pl.ds(0, (n_tok - 1) * block), :])
         x, gated = mix_tokens(s)
-        project(s, (gated * gain).astype(BF16))
+        def between(ch, s=s):
+            if s > 0 and ch + WEAVE < chunks:
+                forward(s - 1, ch + WEAVE)
+
+        project(s, (gated * gain).astype(BF16), between)
         spread(s, gated)
         commit(s, x)
+        if s in EARLY:
+            hand_out(s)
+        if s + 1 < seqs:
+            prepare(s + 1)
+        for ch in range(chunks if s == seqs - 1 else min(WEAVE, chunks)):
+            forward(s, ch)
+
+    narrow = []
+    for s in range(seqs):
+        take(ss_recv.at[s], ss_l.at[s, pl.ds(0, group - 1)])
+        sources = [lax.rem(head - o + n_head, n_head) for o in range(n_head)]
+        places = [(head * lines + l) * 2 + lax.rem(side + line + l, 2) for l in range(lines)]
+        wide = None
+        if "B" in plan[s]:
+            wide = [[factor(s, source, at) for at in places] for source in sources]
+        near = {}
+        if "A" in plan[s]:
+            near["A"] = [factor(s, source, me) for source in sources]
+        narrow.append(near)
         for ch in range(chunks):
-            forward(s, ch)
+            second(s, ch, wide)
+        if s == LATE:
+            for later in range(seqs):
+                if later not in EARLY:
+                    hand_out(later)
 
     take(got.at[0], n_l.at[pl.ds(0, n_tok - 1)])
     take(got.at[1], stat_l.at[pl.ds(0, n_tok - 1)])
-    lanes = iota((m_own, m_pair), 1)
-    r = iota((m_own, m_pair), 0)
-    want = None
-    for h in range(per_kv):
-        t = r - h * block
-        hit = (t >= 0) & (t < block) & (lanes == h * pair + side * block + t)
-        want = hit if want is None else want | hit
     for s in range(seqs):
         levels = [
-            jnp.sum(jnp.where(want, stat_l[t, s : s + 1, :], 0.0), axis=1, keepdims=True)
+            jnp.sum(jnp.where(eye, stat_l[t, s], 0.0), axis=1, keepdims=True)
             for t in range(n_tok)
         ]
         top = functools.reduce(jnp.maximum, levels)
@@ -410,16 +453,6 @@
         for h in range(per_kv):
             ctx_ref[s, :, h * att : (h + 1) * att] = acc[h * block : (h + 1) * block]
 
-    narrow = []
-    for s in range(seqs):
-        take(ss_recv.at[s], ss_l.at[s, pl.ds(0, group - 1)])
-        sources = [lax.rem(head - o + n_head, n_head) for o in range(n_head)]
-        places = [(head * lines + l) * 2 + lax.rem(side + line + l, 2) for l in range(lines)]
-        wide = [[factor(s, source, at) for at in places] for source in sources]
-        narrow.append([factor(s, source, me) for source in sources])
-        for ch in range(chunks):
-            second(s, ch, wide)
-
     take(got.at[2], cm_l.at[:, :, pl.ds(0, (n_tok - 1) * width)])
     for s in range(seqs):
         for h in range(heads):
@@ -431,7 +464,7 @@
         weave = jnp.where(at == (of - s * per) * seqs + s, jnp.where((of >= s * per) & (of < (s + 1) * per), 1.0, weave), weave)
     weave = weave.astype(BF16)
     for ch in range(chunks):
-        both = jnp.concatenate([final(s, ch, narrow[s]) for s in range(seqs)], axis=0)
+        both = jnp.concatenate([final(s, ch, narrow[s].get(plan[s][ch])) for s in range(seqs)], axis=0)
         both = dot(weave, both.astype(BF16)).astype(BF16)
         for d in range(per):
             out_ref[d, :, piece_of(ch)] = both[d * seqs : (d + 1) * seqs]
@@ -440,7 +473,6 @@
     most = pl.ds(0, (n_tok - 1) * block)
     take(sent.at[0], q_l.at[:, most, :])
     take(sent.at[1], bc_l.at[:, :, most, :])
-    take(sent.at[2], dt_l.at[:, most, :])
     take(sent.at[3], turn_v.at[:, :, pl.ds(0, (n_tok - 1) * width)])
     take(sent.at[4], xz_v.at[:, :, :, pl.ds(0, (n_tok - 1) * width)])
     take(sent.at[5], n_s.at[others])
@@ -448,11 +480,15 @@
     take(sent.at[7], ss_l.at[:, pl.ds(0, group - 1)])
     take(sent.at[8], pair_l)
     take(sent.at[9], cm_s.at[:, pl.ds(0, (n_tok - 1) * cols), :])
-    partial = pl.ds(0, out_cols // 2)
-    take(sent.at[10], one_a.at[:, pl.ds(1, lines - 1), :, :, partial])
-    take(sent.at[11], one_b.at[:, pl.ds(1, n_head - 1), :, :, partial])
-    take(sent.at[12], two_a.at[:, pl.ds(1, n_head - 1), :, partial])
-    take(sent.at[13], two_b.at[:, pl.ds(1, lines - 1), :, partial])
+    for k, share_of in enumerate(sorted(set(counts))):
+        same = pl.ds(counts.index(share_of), counts.count(share_of))
+        a, b = pl.ds(0, share_of * span), pl.ds(0, (chunks - share_of) * span)
+        if share_of:
+            take(sent.at[10 + 4 * k], one_a.at[same, pl.ds(1, lines - 1), :, :, a])
+            take(sent.at[12 + 4 * k], two_a.at[same, pl.ds(1, n_head - 1), :, a])
+        if share_of < chunks:
+            take(sent.at[11 + 4 * k], one_b.at[same, pl.ds(1, n_head - 1), :, :, b])
+            take(sent.at[13 + 4 * k], two_b.at[same, pl.ds(1, lines - 1), :, b])
 
 
 def finish(out_v, ctx_v, com_v, out_ref, ctx_ref, com_ref, sems):
@@ -487,7 +523,8 @@
     cache = cached_key_rows.shape[1]
     out_cols = out_weight.shape[1]
     per = draft // group
-    chunks = 4
+    plan = [PLAN[min(s, len(PLAN) - 1)] for s in range(seqs)]
+    chunks = len(plan[0])
     hops = max(lines, n_head) - 1
     turned = jnp.transpose(ssm_state, (0, 1, 3, 2))
     shapes = (
@@ -502,15 +539,15 @@
     )
     vmem = pl.BlockSpec(memory_space=pltpu.VMEM)
     held = pl.pallas_call(
-        functools.partial(kernel, (n_head, n_tok, seqs, block, heads, chunks)),
+        functools.partial(kernel, (n_head, n_tok, seqs, block, heads, plan)),
         out_shape=[pltpu.VMEM(shape, BF16) for shape in shapes],
         in_specs=[pl.BlockSpec(memory_space=pltpu.HBM)] * len(operands),
         out_specs=[vmem] * 3,
         scratch_shapes=[
             pltpu.VMEM((seqs, 2, block, features), BF16),
             pltpu.VMEM((seqs, 2, draft, width), BF16),
-            pltpu.VMEM((2, seqs, draft, state), BF16),
-            pltpu.VMEM((seqs, draft, heads), BF16),
+            pltpu.VMEM((3, seqs, draft, state), BF16),
+            pltpu.VMEM((seqs, block, heads), BF16),
             pltpu.VMEM((seqs, heads, cols, size), BF16),
             pltpu.VMEM((seqs, cols, features), BF16),
             pltpu.VMEM((seqs, state, width), BF16),
@@ -524,8 +561,8 @@
             pltpu.VMEM((seqs, cols, features), BF16),
             pltpu.VMEM((n_tok, seqs, per_kv * block, att), BF16),
             pltpu.VMEM((n_tok, seqs, per_kv * block, att), BF16),
-            pltpu.VMEM((lines, seqs, 2 * per_kv * block), F32),
-            pltpu.VMEM((n_tok, seqs, 2 * per_kv * block), F32),
+            pltpu.VMEM((n_tok, seqs, 1, per_kv * block), F32),
+            pltpu.VMEM((n_tok, seqs, 1, per_kv * block), F32),
             pltpu.VMEM((seqs, 2, n_head, lines, per, out_cols), BF16),
             pltpu.VMEM((seqs, n_head, lines, per, out_cols), BF16),
             pltpu.VMEM((seqs, n_head, lines, per, out_cols), BF16),
@@ -535,13 +572,10 @@
             pltpu.VMEM((seqs, lines, per, out_cols), BF16),
             pltpu.VMEM((seqs, n_head, per, out_cols), BF16),
             pltpu.VMEM((seqs, lines, per, out_cols), BF16),
-            pltpu.SMEM(decay_rate.shape, F32),
-            pltpu.SMEM(skip_weight.shape, F32),
-            pltpu.SMEM(cache_len.shape, jnp.int32),
-            pltpu.SMEM(accepted.shape, jnp.int32),
-            pltpu.SemaphoreType.DMA((14,)),
+            pltpu.SMEM((2,) + decay_rate.shape, F32),
+            pltpu.SMEM((2,) + cache_len.shape, jnp.int32),
+            pltpu.SemaphoreType.DMA((10 + 4 * len({row.count("A") for row in plan}),)),
             pltpu.SemaphoreType.DMA((n_tok - 1,)),
-            pltpu.SemaphoreType.DMA((lines,)),
             pltpu.SemaphoreType.DMA((lines,)),
             pltpu.SemaphoreType.DMA((seqs,)),
             pltpu.SemaphoreType.DMA((seqs,)),
@@ -550,7 +584,7 @@
             pltpu.SemaphoreType.DMA((seqs, chunks)),
             pltpu.SemaphoreType.DMA((seqs, chunks, hops)),
             pltpu.SemaphoreType.DMA((seqs, chunks, hops)),
-            pltpu.SemaphoreType.DMA((13,)),
+            pltpu.SemaphoreType.DMA((11,)),
         ],
         compiler_params=pltpu.CompilerParams(
             collective_id=0, has_side_effects=True, vmem_limit_bytes=40 * 1024 * 1024

time: 21 us -> 19.8 us (0.943)
  Pallas kernels: 20.2 us -> 19 us
    pallas_call x1, Pallas kernels: 19.4 us -> 18.3 us  [body(): pl.pallas_call(functools.partial(kernel, (n_head, n_tok, seqs, block, hea...]
where the time goes in v4:
time: 19.8 us; the launch traced here: 19.7 us
  Pallas kernels  19 us (96%)
  between operations  0.65 us (3%)
    pallas_call x1, Pallas kernels, body(): pl.pallas_call(functools.partial(kernel, (n_head, n_tok, seqs, block, hea...  18.3 us
    pallas_call x1, Pallas kernels, body(): pl.pallas_call(finish, out_shape=[jax.ShapeDtypeStruct(shape, BF16) for s...  0.78 us

profile of v4, /device:TPU:0, one launch (start us, length us, event | category | flops | bytes accessed | tf_op | source)
XLA Modules:
  0.0 19.7 jit_solution(10310060953342075650)
XLA Ops:
  0.6 18.3 %hybrid.1 = (bf16[8,2,4096]{2,1,0:T(2,128)(2,1)S(1)}, bf16[2,16,512]{2,1,0:T(8,128)(2,1)S(1)}, bf16[2,16,32,64]{3,2,1,0:T(8,128)(2,1)S(1)}) custom-call(bf16[2,16,1024]{2,1,0:T(8,128)(2,1)} %x_in.1, bf16[2,16,1024]{2,1,0:T(8,128)(2,1)} %z_in.1, bf16[2,16,128]{2,1,0:T(8,128)(2,1)} %b_in.1, bf16[2,16,128]{2,1,0:T(8,128)(2,1)} %c_in.1, ...), custom_call_target="tpu_custom_call" | custom-call | tf_op jit(solution)/shard_map/hybrid/pallas_call | solution.py:541
  18.9 0.8 %finish.1 = (bf16[8,2,4096]{2,1,0:T(2,128)(2,1)}, bf16[2,16,512]{2,1,0:T(8,128)(2,1)}, bf16[2,16,32,64]{3,2,1,0:T(8,128)(2,1)}) custom-call(bf16[8,2,4096]{2,1,0:T(2,128)(2,1)S(1)} %get-tuple-element.9.out_v, bf16[2,16,512]{2,1,0:T(8,128)(2,1)S(1)} %get-tuple-element.10.ctx_v, bf16[2,16,32,64]{3,2,1,0:T(8,128)(2,1)S(1)} %get-tuple-element.11.com_v), custom_call_target="tpu_custom_call" | custom-call | tf_op jit(solution)/shard_map/finish/pallas_call | solution.py:594

commit v5 on v4

--- a/solution.py
+++ b/solution.py
@@ -27,6 +27,9 @@
 EARLY = (0,)
 LATE = 0
 WEAVE = 2
+FIRST = 0
+POWER = False
+LOG2E = 1.4426950408889634
 
 
 def kernel(
@@ -183,25 +186,41 @@
                 hit = (t >= 0) & (t < block) & (lanes == h * block + t)
                 pick = hit if pick is None else pick | hit
             picks.append(pick)
-        for s in range(seqs):
-            q = jnp.concatenate(
+        each = range(seqs)
+        q = [
+            jnp.concatenate(
                 [q_l[s, place(at, height), h * att : (h + 1) * att] for h in range(per_kv)], axis=0
             )
-            old = lax.dot_general(q, kv_v[0, s], NT, preferred_element_type=F32)
-            old = jnp.where(position < seqs_ref[0, s], old, MASKED)
-            new = lax.dot_general(q, new_v[0, s], NT, preferred_element_type=F32)
-            new = jnp.where(inner <= (first - tok) * block, new, MASKED)
-            peak = jnp.maximum(
-                jnp.max(old, axis=1, keepdims=True), jnp.max(new, axis=1, keepdims=True)
+            for s in each
+        ]
+        old = [lax.dot_general(q[s], kv_v[0, s], NT, preferred_element_type=F32) for s in each]
+        new = [lax.dot_general(q[s], new_v[0, s], NT, preferred_element_type=F32) for s in each]
+        old = [jnp.where(position < seqs_ref[0, s], old[s], MASKED) for s in each]
+        new = [jnp.where(inner <= (first - tok) * block, new[s], MASKED) for s in each]
+        peak = [
+            jnp.maximum(
+                jnp.max(old[s], axis=1, keepdims=True), jnp.max(new[s], axis=1, keepdims=True)
             )
-            peak = jnp.maximum(peak, FLOOR)
-            old = jnp.exp((old - peak) * scale)
-            new = jnp.exp((new - peak) * scale)
-            total = jnp.sum(old, axis=1, keepdims=True) + jnp.sum(new, axis=1, keepdims=True)
-            numer = dot(old.astype(BF16), kv_v[1, s]) + dot(new.astype(BF16), new_v[1, s])
-            safe = jnp.maximum(total, 1e-30)
-            level = jnp.where(total > 0.0, peak * scale + jnp.log(safe), MASKED)
-            ctx = (numer / safe).astype(BF16)
+            for s in each
+        ]
+        peak = [jnp.maximum(peak[s], FLOOR) for s in each]
+        if POWER:
+            lift = [peak[s] * (scale * LOG2E) for s in each]
+            old = [jnp.exp2(old[s] * (scale * LOG2E) - lift[s]) for s in each]
+            new = [jnp.exp2(new[s] * (scale * LOG2E) - lift[s]) for s in each]
+        else:
+            old = [jnp.exp((old[s] - peak[s]) * scale) for s in each]
+            new = [jnp.exp((new[s] - peak[s]) * scale) for s in each]
+        numer = [dot(old[s].astype(BF16), kv_v[1, s]) for s in each]
+        numer = [numer[s] + dot(new[s].astype(BF16), new_v[1, s]) for s in each]
+        total = [
+            jnp.sum(old[s], axis=1, keepdims=True) + jnp.sum(new[s], axis=1, keepdims=True)
+            for s in each
+        ]
+        for s in each:
+            safe = jnp.maximum(total[s], 1e-30)
+            level = jnp.where(total[s] > 0.0, peak[s] * scale + jnp.log(safe), MASKED)
+            ctx = (numer[s] / safe).astype(BF16)
             for c in range(count):
                 for h in range(per_kv):
                     n_s[first + c, s, h * block : (h + 1) * block] = ctx[
@@ -278,7 +297,7 @@
         inside = dot(mix, (x * shrunk).astype(BF16))
         y = grown * (inside + dot(bc_l[1, s], st_l[s])) + skip_x * x
         gated = y * z / (1.0 + jnp.exp(-z))
-        return x, gated
+        return gated
 
     def spread(s, gated):
         sums = jnp.sum(gated * gated, axis=1, keepdims=True)
@@ -307,7 +326,8 @@
             )
             between(ch)
 
-    def commit(s, x):
+    def commit(s):
+        x = xz_l[s, 0].astype(F32)
         weight, decay, flow = early[s][3:]
         new = decay * st_l[s].astype(F32) + dot(flow, (x * weight).astype(BF16))
         cm_s[s] = new.astype(BF16)
@@ -402,20 +422,30 @@
     for s in range(seqs):
         take(st_recv.at[s], st_l.at[s, pl.ds(0, (n_tok - 1) * cols), :])
         take(xz_recv.at[s], xz_l.at[s, :, pl.ds(0, (n_tok - 1) * block), :])
-        x, gated = mix_tokens(s)
+        if FIRST == 0 and s in EARLY:
+            commit(s)
+            hand_out(s)
+        gated = mix_tokens(s)
+
         def between(ch, s=s):
             if s > 0 and ch + WEAVE < chunks:
                 forward(s - 1, ch + WEAVE)
 
         project(s, (gated * gain).astype(BF16), between)
         spread(s, gated)
-        commit(s, x)
-        if s in EARLY:
-            hand_out(s)
+        if s not in EARLY or FIRST > 0:
+            commit(s)
+            if s in EARLY and FIRST == 1:
+                hand_out(s)
         if s + 1 < seqs:
             prepare(s + 1)
         for ch in range(chunks if s == seqs - 1 else min(WEAVE, chunks)):
             forward(s, ch)
+        if FIRST == 3 and s in EARLY:
+            hand_out(s)
+    for s in range(seqs):
+        if FIRST == 2 and s in EARLY:
+            hand_out(s)
 
     narrow = []
     for s in range(seqs):

time: 19.8 us -> 19.9 us (level)
  no operation moved by 1% of the time
where the time goes in v5:
time: 19.9 us; the launch traced here: 19.8 us
  Pallas kernels  19.1 us (96%)
  between operations  0.65 us (3%)
    pallas_call x1, Pallas kernels, body(): pl.pallas_call(functools.partial(kernel, (n_head, n_tok, seqs, block, hea...  18.4 us
    pallas_call x1, Pallas kernels, body(): pl.pallas_call(finish, out_shape=[jax.ShapeDtypeStruct(shape, BF16) for s...  0.78 us

profile of v5, /device:TPU:0, one launch (start us, length us, event | category | flops | bytes accessed | tf_op | source)
XLA Modules:
  0.0 19.8 jit_solution(667377494111045632)
XLA Ops:
  0.6 18.4 %hybrid.1 = (bf16[8,2,4096]{2,1,0:T(2,128)(2,1)S(1)}, bf16[2,16,512]{2,1,0:T(8,128)(2,1)S(1)}, bf16[2,16,32,64]{3,2,1,0:T(8,128)(2,1)S(1)}) custom-call(bf16[2,16,1024]{2,1,0:T(8,128)(2,1)} %x_in.1, bf16[2,16,1024]{2,1,0:T(8,128)(2,1)} %z_in.1, bf16[2,16,128]{2,1,0:T(8,128)(2,1)} %b_in.1, bf16[2,16,128]{2,1,0:T(8,128)(2,1)} %c_in.1, ...), custom_call_target="tpu_custom_call" | custom-call | tf_op jit(solution)/shard_map/hybrid/pallas_call | solution.py:571
  19.0 0.8 %finish.1 = (bf16[8,2,4096]{2,1,0:T(2,128)(2,1)}, bf16[2,16,512]{2,1,0:T(8,128)(2,1)}, bf16[2,16,32,64]{3,2,1,0:T(8,128)(2,1)}) custom-call(bf16[8,2,4096]{2,1,0:T(2,128)(2,1)S(1)} %get-tuple-element.9.out_v, bf16[2,16,512]{2,1,0:T(8,128)(2,1)S(1)} %get-tuple-element.10.ctx_v, bf16[2,16,32,64]{3,2,1,0:T(8,128)(2,1)S(1)} %get-tuple-element.11.com_v), custom_call_target="tpu_custom_call" | custom-call | tf_op jit(solution)/shard_map/finish/pallas_call | solution.py:624

commit v6 on v5

--- a/solution.py
+++ b/solution.py
@@ -386,7 +386,7 @@
                 to = lax.rem(head + o, n_head)
                 remote(
                     12 + 4 * kinds[s], mid_a.at[s, to, :, piece], two_a.at[s, o, :, piece],
-                    two_recv.at[s, ch, o - 1], above(o),
+                    two_recv.at[s, 0, o - 1], above(o),
                 )
         else:
             for o in range(1, n_head):
@@ -400,20 +400,16 @@
                 to = lax.rem(line + o, lines)
                 remote(
                     13 + 4 * kinds[s], mid_b.at[s, to, :, piece], two_b.at[s, o, :, piece],
-                    two_recv.at[s, ch, o - 1], {"tok": across(o)},
+                    two_recv.at[s, 1, o - 1], {"tok": across(o)},
                 )
 
     def final(s, ch, factors):
         piece = piece_of(ch)
         if plan[s][ch] == "A":
-            for o in range(1, n_head):
-                take(two_recv.at[s, ch, o - 1], two_a.at[s, o, :, piece])
             total = mid_a[s, head, :, piece].astype(F32) * factors[0]
             for o in range(1, n_head):
                 total = total + two_a[s, o, :, piece].astype(F32) * factors[o]
         else:
-            for o in range(1, lines):
-                take(two_recv.at[s, ch, o - 1], two_b.at[s, o, :, piece])
             total = mid_b[s, line, :, piece].astype(F32)
             for o in range(1, lines):
                 total = total + two_b[s, o, :, piece].astype(F32)
@@ -493,6 +489,14 @@
     for s in range(seqs):
         weave = jnp.where(at == (of - s * per) * seqs + s, jnp.where((of >= s * per) & (of < (s + 1) * per), 1.0, weave), weave)
     weave = weave.astype(BF16)
+    for s in range(seqs):
+        a, b = pl.ds(0, counts[s] * span), pl.ds(0, (chunks - counts[s]) * span)
+        if counts[s]:
+            for o in range(1, n_head):
+                take(two_recv.at[s, 0, o - 1], two_a.at[s, o, :, a])
+        if counts[s] < chunks:
+            for o in range(1, lines):
+                take(two_recv.at[s, 1, o - 1], two_b.at[s, o, :, b])
     for ch in range(chunks):
         both = jnp.concatenate([final(s, ch, narrow[s].get(plan[s][ch])) for s in range(seqs)], axis=0)
         both = dot(weave, both.astype(BF16)).astype(BF16)
@@ -613,7 +617,7 @@
             pltpu.SemaphoreType.DMA((seqs,)),
             pltpu.SemaphoreType.DMA((seqs, chunks)),
             pltpu.SemaphoreType.DMA((seqs, chunks, hops)),
-            pltpu.SemaphoreType.DMA((seqs, chunks, hops)),
+            pltpu.SemaphoreType.DMA((seqs, 2, hops)),
             pltpu.SemaphoreType.DMA((11,)),
         ],
         compiler_params=pltpu.CompilerParams(

time: 19.9 us -> 20 us (level)
  no operation moved by 1% of the time
where the time goes in v6:
time: 20 us; the launch traced here: 19.8 us
  Pallas kernels  19.2 us (96%)
  between operations  0.65 us (3%)
    pallas_call x1, Pallas kernels, body(): pl.pallas_call(functools.partial(kernel, (n_head, n_tok, seqs, block, hea...  18.4 us
    pallas_call x1, Pallas kernels, body(): pl.pallas_call(finish, out_shape=[jax.ShapeDtypeStruct(shape, BF16) for s...  0.78 us

profile of v6, /device:TPU:0, one launch (start us, length us, event | category | flops | bytes accessed | tf_op | source)
XLA Modules:
  0.0 19.8 jit_solution(8837021335717829749)
XLA Ops:
  0.6 18.4 %hybrid.1 = (bf16[8,2,4096]{2,1,0:T(2,128)(2,1)S(1)}, bf16[2,16,512]{2,1,0:T(8,128)(2,1)S(1)}, bf16[2,16,32,64]{3,2,1,0:T(8,128)(2,1)S(1)}) custom-call(bf16[2,16,1024]{2,1,0:T(8,128)(2,1)} %x_in.1, bf16[2,16,1024]{2,1,0:T(8,128)(2,1)} %z_in.1, bf16[2,16,128]{2,1,0:T(8,128)(2,1)} %b_in.1, bf16[2,16,128]{2,1,0:T(8,128)(2,1)} %c_in.1, ...), custom_call_target="tpu_custom_call" | custom-call | tf_op jit(solution)/shard_map/hybrid/pallas_call | solution.py:575
  19.0 0.8 %finish.1 = (bf16[8,2,4096]{2,1,0:T(2,128)(2,1)}, bf16[2,16,512]{2,1,0:T(8,128)(2,1)}, bf16[2,16,32,64]{3,2,1,0:T(8,128)(2,1)}) custom-call(bf16[8,2,4096]{2,1,0:T(2,128)(2,1)S(1)} %get-tuple-element.9.out_v, bf16[2,16,512]{2,1,0:T(8,128)(2,1)S(1)} %get-tuple-element.10.ctx_v, bf16[2,16,32,64]{3,2,1,0:T(8,128)(2,1)S(1)} %get-tuple-element.11.com_v), custom_call_target="tpu_custom_call" | custom-call | tf_op jit(solution)/shard_map/finish/pallas_call | solution.py:628
